TPU v7x, 32 devices: a whole 2x2x4 slice. The times are simulated.
32 devices in a mesh: batch: 4 (over x, core), row: 2 (over y), col: 4 (over z).
Axes of the slice: x: 2, y: 2, z: 4, core: 2. Of those that a mesh axis runs over, the one named last changes fastest.
Arguments:
- inputs: float32 [8192, 1536], P(('batch', 'col'), 'row'), may hold values from -8 to 8
- segments: int32 [16, 512], P(('batch', 'row')), may hold values from 0 to 511, as said below
- positions: int32 [16, 512], P(('batch', 'row')), may hold values from 0 to 2558, as said below
- gain_attn: float32 [1536], P('row'), may hold values from 0.5 to 1.5
- gain_mlp: float32 [1536], P('row'), may hold values from 0.5 to 1.5
- w_qkv: bfloat16 [1536, 1536], P('row', 'col'), may hold values from -0.19385052 to 0.19385052
- w_out: bfloat16 [768, 1536], P('col', 'row'), may hold values from -1.25 to 1.25
- w_gate: bfloat16 [1536, 4096], P('row', 'col'), may hold values from -0.15625 to 0.15625
- w_up: bfloat16 [1536, 4096], P('row', 'col'), may hold values from -0.15625 to 0.15625
- w_down: bfloat16 [4096, 1536], P('col', 'row'), may hold values from -0.09375 to 0.09375
- grad_output: float32 [8192, 1536], P(('batch', 'col'), 'row'), may hold values from -6 to 6
Outputs:
- result: float32 [8192, 1536], P(('batch', 'col'), 'row')
- grad_inputs: float32 [8192, 1536], P(('batch', 'col'), 'row')
- grad_gain_attn: float32 [1536], P('row')
- grad_gain_mlp: float32 [1536], P('row')
- grad_w_qkv: float32 [1536, 1536], P('row', 'col')
- grad_w_out: float32 [768, 1536], P('col', 'row')
- grad_w_gate: float32 [1536, 4096], P('row', 'col')
- grad_w_up: float32 [1536, 4096], P('row', 'col')
- grad_w_down: float32 [4096, 1536], P('col', 'row')
Inputs may be any that keep to these rules, and one draw needn't show every extreme that they name: `segments`: in each packed row the segment numbers start at 0 and never fall. `positions`: inside a segment the position rises by one from token to token.
All inputs are finite; a program needn't handle non-finite values.
Results may differ from a plain program's by a relative error of at most 0.015.
The roundings to bfloat16 on the way count: a program that leaves them out, or rounds other values in their place, can miss the bound.
Values may be sent and summed in bfloat16 or wider, within the bound.
A program may use at most 192 MiB of HBM per device.

v0:
```python
import math

import jax
import jax.numpy as jnp
from jax import lax
from jax.sharding import PartitionSpec as P

D = 1536


EPS = 1e-05
ROPE_BASE = 100000.0
NEG_FILL = -1e30


def token_stats(values):
    return lax.psum(values, "row")


def widen(tensor):
    return lax.all_gather(tensor, "col", axis=0, tiled=True)


def narrow_sum(partial_sum):
    return lax.psum_scatter(partial_sum, "col", scatter_dimension=0, tiled=True)


def rows_sum(partial_sum):
    return lax.psum_scatter(partial_sum, "row", scatter_dimension=0, tiled=True)


def rows_gather(tensor):
    return lax.all_gather(tensor, "row", axis=0, tiled=True)


def norm_forward(values, gain_vec):
    totals = token_stats(jnp.sum(values * values, axis=1))
    inverse = lax.rsqrt(totals / D + EPS)[:, None]
    normed = values * inverse
    return (normed, inverse, (normed * gain_vec).astype(jnp.bfloat16))


def norm_backward(upstream, grad_hidden, normed, inverse, gain_vec):
    scaled = grad_hidden * gain_vec
    totals = token_stats(jnp.sum(scaled * normed, axis=1))
    centre = (totals / D)[:, None]
    return (upstream + inverse * (scaled - normed * centre), jnp.sum(grad_hidden * normed, axis=0))


def rope_tables(positions, head_size):
    half_size = head_size // 2
    frequency = ROPE_BASE ** (-(jnp.arange(half_size, dtype=jnp.float32) * 2.0 / head_size))
    angles = positions.astype(jnp.float32)[..., None] * frequency
    return (jnp.cos(angles), jnp.sin(angles))


def rotate(tensor, cosine_table, sine_table):
    half_size = tensor.shape[-1] // 2
    front_half = tensor[..., :half_size]
    back_half = tensor[..., half_size:]
    return jnp.concatenate(
        [
            front_half * cosine_table - back_half * sine_table,
            back_half * cosine_table + front_half * sine_table,
        ],
        axis=-1,
    )


def masked_scores(rotary_queries, rotary_keys, segments, score_scale):
    scores = (
        jnp.einsum(
            "nyrw,nzw->nryz", rotary_queries, rotary_keys, preferred_element_type=jnp.float32
        )
        * score_scale
    )
    order = jnp.arange(segments.shape[1])
    allowed = (segments[:, :, None] == segments[:, None, :]) & (order[:, None] >= order[None, :])[
        None
    ]
    return jnp.where(allowed[:, None], scores, NEG_FILL)


def attend_forward(rotary_queries, rotary_keys, value_matrix, segments, score_scale):
    scores = masked_scores(rotary_queries, rotary_keys, segments, score_scale)
    row_max = jnp.max(scores, axis=-1, keepdims=True)
    log_total = row_max + jnp.log(jnp.sum(jnp.exp(scores - row_max), axis=-1, keepdims=True))
    attention_weight_matrix = jnp.exp(scores - log_total).astype(jnp.bfloat16)
    attention_output = jnp.einsum(
        "uoap,upy->uaoy", attention_weight_matrix, value_matrix, preferred_element_type=jnp.float32
    )
    return (attention_output.astype(jnp.bfloat16), log_total)


def attend_backward(
    rotary_queries,
    rotary_keys,
    value_matrix,
    segments,
    log_total,
    attention_output_gradient,
    score_scale,
):
    scores = masked_scores(rotary_queries, rotary_keys, segments, score_scale)
    weights_f = jnp.exp(scores - log_total)
    grad_probs = jnp.einsum(
        "nyrw,nzw->nryz",
        attention_output_gradient,
        value_matrix,
        preferred_element_type=jnp.float32,
    )
    centre = jnp.sum(weights_f * grad_probs, axis=-1, keepdims=True)
    score_gradient = (weights_f * (grad_probs - centre)).astype(jnp.bfloat16)
    grad_qrot = (
        jnp.einsum(
            "uoap,upy->uaoy", score_gradient, rotary_keys, preferred_element_type=jnp.float32
        )
        * score_scale
    )
    grad_krot = (
        jnp.einsum(
            "ynep,yeno->ypo", score_gradient, rotary_queries, preferred_element_type=jnp.float32
        )
        * score_scale
    )
    grad_value = jnp.einsum(
        "ynep,yeno->ypo",
        weights_f.astype(jnp.bfloat16),
        attention_output_gradient,
        preferred_element_type=jnp.float32,
    )
    return (grad_qrot, grad_krot, grad_value)


def matmul(left, right):
    return jnp.dot(left, right, preferred_element_type=jnp.float32)


def left_t(left, right):
    return jnp.einsum("ta,tb->ab", left, right, preferred_element_type=jnp.float32)


def right_t(left, right):
    return jnp.einsum("tb,ab->ta", left, right, preferred_element_type=jnp.float32)


def shards(
    inputs,
    segments,
    positions,
    gain_attn,
    gain_mlp,
    w_qkv,
    w_out,
    w_gate,
    w_up,
    w_down,
    grad_output,
):
    bf = jnp.bfloat16
    seq_count, seq_len = segments.shape
    query_cols = w_out.shape[0]
    head_size = w_qkv.shape[1] - query_cols - (w_qkv.shape[1] - query_cols) // 2
    group_heads = query_cols // head_size
    local_tokens = seq_count * seq_len
    ff_cols = w_gate.shape[1]
    score_scale = 1.0 / math.sqrt(head_size)
    cosine_table, sine_table = rope_tables(positions, head_size)
    normed_one, inverse_one, hidden_one = norm_forward(inputs, gain_attn)
    wide_one = widen(hidden_one)
    qkv_local = rows_sum(matmul(wide_one, w_qkv))
    queries = qkv_local[:, :query_cols].reshape(seq_count, seq_len, group_heads, head_size)
    key_part = qkv_local[:, query_cols : query_cols + head_size].reshape(
        seq_count, seq_len, head_size
    )
    value_matrix = (
        qkv_local[:, query_cols + head_size :].reshape(seq_count, seq_len, head_size).astype(bf)
    )
    rotary_queries = rotate(queries, cosine_table[:, :, None, :], sine_table[:, :, None, :]).astype(
        bf
    )
    rotary_keys = rotate(key_part, cosine_table, sine_table).astype(bf)
    attention_output, log_total = attend_forward(
        rotary_queries, rotary_keys, value_matrix, segments, score_scale
    )
    attended_flat = attention_output.reshape(local_tokens, query_cols)
    wide_attended = rows_gather(attended_flat)
    mixed_in = inputs + narrow_sum(matmul(wide_attended, w_out))
    normed_two, inverse_two, hidden_two = norm_forward(mixed_in, gain_mlp)
    wide_two = widen(hidden_two)
    gate_up = rows_sum(jnp.concatenate([matmul(wide_two, w_gate), matmul(wide_two, w_up)], axis=1))
    gate_vals = gate_up[:, :ff_cols]
    up_vals = gate_up[:, ff_cols:]
    gate_sigmoid = jax.nn.sigmoid(gate_vals)
    activated = (gate_vals * gate_sigmoid * up_vals).astype(bf)
    wide_act = rows_gather(activated)
    result = mixed_in + narrow_sum(matmul(wide_act, w_down))
    grad_wide = widen(grad_output.astype(bf))
    grad_w_down = left_t(wide_act, grad_wide)
    grad_act = rows_sum(right_t(grad_wide, w_down))
    grad_gate = (
        grad_act * up_vals * gate_sigmoid * (1.0 + gate_vals * (1.0 - gate_sigmoid))
    ).astype(bf)
    grad_up = (grad_act * gate_vals * gate_sigmoid).astype(bf)
    wide_grads = rows_gather(jnp.concatenate([grad_gate, grad_up], axis=1))
    grad_w_gate = left_t(wide_two, wide_grads[:, :ff_cols])
    grad_w_up = left_t(wide_two, wide_grads[:, ff_cols:])
    grad_hidden_two = narrow_sum(
        right_t(wide_grads[:, :ff_cols], w_gate) + right_t(wide_grads[:, ff_cols:], w_up)
    )
    grad_mixed, grad_gain_mlp = norm_backward(
        grad_output, grad_hidden_two, normed_two, inverse_two, gain_mlp
    )
    grad_mixed_wide = widen(grad_mixed.astype(bf))
    grad_w_out = left_t(wide_attended, grad_mixed_wide)
    attention_output_gradient = (
        rows_sum(right_t(grad_mixed_wide, w_out))
        .astype(bf)
        .reshape(seq_count, seq_len, group_heads, head_size)
    )
    grad_qrot, grad_krot, grad_value = attend_backward(
        rotary_queries,
        rotary_keys,
        value_matrix,
        segments,
        log_total,
        attention_output_gradient,
        score_scale,
    )
    grad_query = rotate(grad_qrot, cosine_table[:, :, None, :], -sine_table[:, :, None, :]).reshape(
        local_tokens, query_cols
    )
    grad_key = rotate(grad_krot, cosine_table, -sine_table).reshape(local_tokens, head_size)
    grad_qkv = jnp.concatenate(
        [grad_query, grad_key, grad_value.reshape(local_tokens, head_size)], axis=1
    ).astype(bf)
    wide_qkv = rows_gather(grad_qkv)
    grad_w_qkv = left_t(wide_one, wide_qkv)
    grad_hidden_one = narrow_sum(right_t(wide_qkv, w_qkv))
    grad_inputs, grad_gain_attn = norm_backward(
        grad_mixed, grad_hidden_one, normed_one, inverse_one, gain_attn
    )
    grad_gain_attn, grad_gain_mlp = lax.psum((grad_gain_attn, grad_gain_mlp), ("batch", "col"))
    grad_w_qkv, grad_w_out, grad_w_gate, grad_w_up, grad_w_down = (
        lax.psum(grad_w_qkv.astype(jnp.bfloat16), "batch").astype(jnp.float32),
        lax.psum(grad_w_out.astype(jnp.bfloat16), "batch").astype(jnp.float32),
        lax.psum(grad_w_gate.astype(jnp.bfloat16), "batch").astype(jnp.float32),
        lax.psum(grad_w_up.astype(jnp.bfloat16), "batch").astype(jnp.float32),
        lax.psum(grad_w_down.astype(jnp.bfloat16), "batch").astype(jnp.float32),
    )
    return (
        result,
        grad_inputs,
        grad_gain_attn,
        grad_gain_mlp,
        grad_w_qkv,
        grad_w_out,
        grad_w_gate,
        grad_w_up,
        grad_w_down,
    )


def solution(mesh):
    return jax.shard_map(
        shards,
        mesh=mesh,
        in_specs=(
            P(("batch", "col"), "row"),
            P(("batch", "row"), None),
            P(("batch", "row"), None),
            P("row"),
            P("row"),
            P("row", "col"),
            P("col", "row"),
            P("row", "col"),
            P("row", "col"),
            P("col", "row"),
            P(("batch", "col"), "row"),
        ),
        out_specs=(
            P(("batch", "col"), "row"),
            P(("batch", "col"), "row"),
            P("row"),
            P("row"),
            P("row", "col"),
            P("col", "row"),
            P("row", "col"),
            P("row", "col"),
            P("col", "row"),
        ),
        check_vma=False,
    )
```

profile of v0, /device:TPU:0, one launch (start us, length us, event | category | flops | bytes accessed | tf_op | source)
XLA Modules:
  0.0 1515.0 jit_solution(12539831173556336820)
XLA Ops:
  17.5 65.3 %all-gather.8.cloned.1.call-done = bf16[2048,768]{1,0:T(8,128)(2,1)} async-done(((bf16[512,768]{1,0:T(8,128)(2,1)}), bf16[2048,768]{1,0:T(8,128)(2,1)}) %all-gather.8.cloned.1.call-update) | async-done | bytes 3145744 | tf_op jit(solution)/shard_map/all_gather | solution.py:21
  89.4 41.0 %reduce-scatter.9.cloned.1.call-done = f32[1024,384]{1,0:T(8,128)} async-done(((f32[2048,384]{1,0:T(8,128)}), f32[1024,384]{1,0:T(8,128)}) %reduce-scatter.9.cloned.1.call-update) | async-done | bytes 1572880 | tf_op jit(solution)/shard_map/reduce_scatter | solution.py:29
  153.0 11.4 all_gather.25
  170.7 108.3 %reduce-scatter.11.cloned.1.call-done = f32[512,768]{1,0:T(8,128)} async-done(((f32[2048,768]{1,0:T(8,128)}), f32[512,768]{1,0:T(8,128)}) %reduce-scatter.11.cloned.1.call-update) | async-done | bytes 1572880 | tf_op jit(solution)/shard_map/reduce_scatter | solution.py:25
  292.4 52.7 %all-gather.14.cloned.1.call-done = bf16[2048,768]{1,0:T(8,128)(2,1)} async-done(((bf16[512,768]{1,0:T(8,128)(2,1)}), bf16[2048,768]{1,0:T(8,128)(2,1)}) %all-gather.14.cloned.1.call-update) | async-done | bytes 3145744 | tf_op jit(solution)/shard_map/all_gather | solution.py:21
  345.0 9.2 fusion.59
  354.3 54.8 %all-gather.10.cloned.1.call-done = bf16[2048,768]{1,0:T(8,128)(2,1)} async-done(((bf16[512,768]{1,0:T(8,128)(2,1)}), bf16[2048,768]{1,0:T(8,128)(2,1)}) %all-gather.10.cloned.1.call-update) | async-done | bytes 3145744 | tf_op jit(solution)/shard_map/all_gather | solution.py:21
  425.2 84.1 %reduce-scatter.17.cloned.1.call-done = f32[1024,1024]{0,1:T(8,128)} async-done(((f32[2048,1024]{0,1:T(8,128)}), f32[1024,1024]{0,1:T(8,128)}) %reduce-scatter.17.cloned.1.call-update) | async-done | bytes 4194320 | tf_op jit(solution)/shard_map/reduce_scatter | solution.py:29
  509.3 191.5 %reduce-scatter.13.cloned.1.call-done = f32[1024,2048]{0,1:T(8,128)} async-done(((f32[2048,2048]{0,1:T(8,128)}), f32[1024,2048]{0,1:T(8,128)}) %reduce-scatter.13.cloned.1.call-update) | async-done | bytes 8388624 | tf_op jit(solution)/shard_map/reduce_scatter | solution.py:29
  700.8 7.0 multiply_convert_fusion.1
  711.3 103.2 %all-gather.16.cloned.1.call-done = bf16[2048,2048]{0,1:T(8,128)(2,1)} async-done(((bf16[1024,2048]{0,1:T(8,128)(2,1)}), bf16[2048,2048]{0,1:T(8,128)(2,1)}) %all-gather.16.cloned.1.call-update) | async-done | bytes 8388624 | tf_op jit(solution)/shard_map/all_gather | solution.py:33
  825.5 47.8 %all-gather.12.cloned.1.call-done = bf16[2048,1024]{0,1:T(8,128)(2,1)} async-done(((bf16[1024,1024]{0,1:T(8,128)(2,1)}), bf16[2048,1024]{0,1:T(8,128)(2,1)}) %all-gather.12.cloned.1.call-update) | async-done | bytes 4194320 | tf_op jit(solution)/shard_map/all_gather | solution.py:33
  873.3 8.5 fusion.58
  881.9 104.4 %reduce-scatter.19.cloned.1.call-done = f32[512,768]{1,0:T(8,128)} async-done(((f32[2048,768]{1,0:T(8,128)}), f32[512,768]{1,0:T(8,128)}) %reduce-scatter.19.cloned.1.call-update) | async-done | bytes 1572880 | tf_op jit(solution)/shard_map/reduce_scatter | solution.py:25
  995.6 104.3 %reduce-scatter.15.cloned.1.call-done = f32[512,768]{1,0:T(8,128)} async-done(((f32[2048,768]{1,0:T(8,128)}), f32[512,768]{1,0:T(8,128)}) %reduce-scatter.15.cloned.1.call-update) | async-done | bytes 1572880 | tf_op jit(solution)/shard_map/reduce_scatter | solution.py:25
  1104.8 64.0 %all-gather.18.cloned.1.call-done = bf16[2048,768]{1,0:T(8,128)(2,1)} async-done(((bf16[512,768]{1,0:T(8,128)(2,1)}), bf16[2048,768]{1,0:T(8,128)(2,1)}) %all-gather.18.cloned.1.call-update) | async-done | bytes 3145744 | tf_op jit(solution)/shard_map/all_gather | solution.py:21
  1173.3 7.7 convolution_convert_fusion
  1181.1 16.9 %reduce-scatter.21.cloned.1.call-done = f32[1024,192]{0,1:T(8,128)} async-done(((f32[2048,192]{0,1:T(8,128)}), f32[1024,192]{0,1:T(8,128)}) %reduce-scatter.21.cloned.1.call-update) | async-done | bytes 786448 | tf_op jit(solution)/shard_map/reduce_scatter | solution.py:29
  1210.8 7.9 fusion.16
  1218.7 7.2 fusion.19
  1227.4 10.4 all-gather.20.cloned.1.call-done
  1250.3 101.2 %all-reduce.4.cloned.1.call-done = (bf16[768,384]{1,0:T(8,128)(2,1)}, bf16[192,768]{1,0:T(8,128)(2,1)}, bf16[768,1024]{1,0:T(8,128)(2,1)}, bf16[768,1024]{1,0:T(8,128)(2,1)}, bf16[1024,768]{1,0:T(8,128)(2,1)}) async-done(((bf16[768,384]{1,0:T(8,128)(2,1)}, bf16[192,768]{1,0:T(8,128)(2,1)}, bf16[768,1024]{1,0:T(8,128)(2,1)}, bf16[768,1024]{1,0:T(8,128)(2,1)}, bf16[1024,768]{1,0:T(8,128)(2,1)}), ...) | async-done | bytes 5603344 | tf_op jit(solution)/shard_map/psum | solution.py:245
  1361.0 103.6 %reduce-scatter.23.cloned.1.call-done = f32[512,768]{1,0:T(8,128)} async-done(((f32[2048,768]{1,0:T(8,128)}), f32[512,768]{1,0:T(8,128)}) %reduce-scatter.23.cloned.1.call-update) | async-done | bytes 1572880 | tf_op jit(solution)/shard_map/reduce_scatter | solution.py:25
  1471.5 33.0 %all-reduce = (f32[768]{0:T(1024)}, f32[768]{0:T(1024)}) all-reduce(f32[768]{0:T(1024)S(1)} %get-tuple-element.11, f32[768]{0:T(1024)S(1)} %copy-done.35), channel_id=1, replica_groups=mesh['batch'=4,'row'=2,'col'=4] {'batch','col'}, use_global_device_ids=true, to_apply=%region_20.21 | all-reduce | flops 1536 | bytes 12288 | tf_op jit(solution)/shard_map/psum | solution.py:243
  (192 shorter events, 154.5 us)
Async XLA Ops:
  7.2 408.1 %copy-start = (bf16[768,1024]{1,0:T(8,128)(2,1)S(1)}, bf16[768,1024]{1,0:T(8,128)(2,1)}, u32[]{:S(2)}) copy-start(bf16[768,1024]{1,0:T(8,128)(2,1)} %param.19) | copy-start | bytes 4718596
  7.2 75.6 %copy-start.22 = (bf16[768,384]{1,0:T(8,128)(2,1)S(1)}, bf16[768,384]{1,0:T(8,128)(2,1)}, u32[]{:S(2)}) copy-start(bf16[768,384]{1,0:T(8,128)(2,1)} %param.16) | copy-start | bytes 1769476
  7.2 75.6 %all-gather.8.cloned.1.call-start = ((), (), s32[]{:S(2)}) async-start(), calls=%async_computation.8 | async-start | bytes 3932160 | tf_op jit(solution)/shard_map/all_gather | solution.py:21
  17.4 113.0 %reduce-scatter.9.cloned.1.call-start = ((), (), s32[]{:S(2)}) async-start(), calls=%async_computation.9 | async-start | bytes 4718592 | tf_op jit(solution)/shard_map/reduce_scatter | solution.py:29
  88.2 190.9 %reduce-scatter.11.cloned.1.call-start = ((), (), s32[]{:S(2)}) async-start(), calls=%async_computation.10 | async-start | bytes 7864320 | tf_op jit(solution)/shard_map/reduce_scatter | solution.py:25
  168.1 110.9 %copy-start.2 = (f32[512,768]{1,0:T(8,128)S(1)}, f32[512,768]{1,0:T(8,128)}, u32[]{:S(2)}) copy-start(f32[512,768]{1,0:T(8,128)} %param.11) | copy-start | bytes 4718596
  168.1 176.9 %all-gather.14.cloned.1.call-start = ((), (), s32[]{:S(2)}) async-start(), calls=%async_computation.15 | async-start | bytes 3932160 | tf_op jit(solution)/shard_map/all_gather | solution.py:21
  170.7 119.0 %copy-start.29 = (f32[768]{0:T(1024)S(1)}, f32[768]{0:T(1024)}, u32[]{:S(2)}) copy-start(f32[768]{0:T(1024)} %param.15) | copy-start | bytes 9220
  170.7 238.5 %all-gather.10.cloned.1.call-start = ((), (), s32[]{:S(2)}) async-start(), calls=%async_computation.11 | async-start | bytes 3932160 | tf_op jit(solution)/shard_map/all_gather | solution.py:21
  292.3 217.0 %reduce-scatter.17.cloned.1.call-start = ((), (), s32[]{:S(2)}) async-start(), calls=%async_computation.16 | async-start | bytes 12582912 | tf_op jit(solution)/shard_map/reduce_scatter | solution.py:29
  354.3 346.5 %reduce-scatter.13.cloned.1.call-start = ((), (), s32[]{:S(2)}) async-start(), calls=%async_computation.12 | async-start | bytes 25165824 | tf_op jit(solution)/shard_map/reduce_scatter | solution.py:29
  425.2 389.3 %all-gather.16.cloned.1.call-start = ((), (), s32[]{:S(2)}) async-start(), calls=%async_computation.17 | async-start | bytes 12582912 | tf_op jit(solution)/shard_map/all_gather | solution.py:33
  710.3 163.0 %all-gather.12.cloned.1.call-start = ((), (), s32[]{:S(2)}) async-start(), calls=%async_computation.13 | async-start | bytes 6291456 | tf_op jit(solution)/shard_map/all_gather | solution.py:33
  711.0 275.2 %reduce-scatter.19.cloned.1.call-start = ((), (), s32[]{:S(2)}) async-start(), calls=%async_computation.18 | async-start | bytes 7864320 | tf_op jit(solution)/shard_map/reduce_scatter | solution.py:25
  825.4 274.5 %reduce-scatter.15.cloned.1.call-start = ((), (), s32[]{:S(2)}) async-start(), calls=%async_computation.14 | async-start | bytes 7864320 | tf_op jit(solution)/shard_map/reduce_scatter | solution.py:25
  881.8 104.5 %copy-start.5 = (f32[512,768]{1,0:T(8,128)S(1)}, f32[512,768]{1,0:T(8,128)}, u32[]{:S(2)}) copy-start(f32[512,768]{1,0:T(8,128)} %get-tuple-element.23) | copy-start | bytes 4718596
  881.8 287.0 %all-gather.18.cloned.1.call-start = ((), (), s32[]{:S(2)}) async-start(), calls=%async_computation.19 | async-start | bytes 3932160 | tf_op jit(solution)/shard_map/all_gather | solution.py:21
  1104.7 93.3 %reduce-scatter.21.cloned.1.call-start = ((), (), s32[]{:S(2)}) async-start(), calls=%async_computation.20 | async-start | bytes 2359296 | tf_op jit(solution)/shard_map/reduce_scatter | solution.py:29
  1173.1 64.7 %all-gather.20.cloned.1.call-start = ((), (), s32[]{:S(2)}) async-start(), calls=%async_computation.21 | async-start | bytes 2359296 | tf_op jit(solution)/shard_map/all_gather | solution.py:33
  1210.5 141.0 %all-reduce.4.cloned.1.call-start = ((), (), s32[]{:S(2)}) async-start(), calls=%async_computation.23 | async-start | bytes 11206656 | tf_op jit(solution)/shard_map/psum | solution.py:245
  1242.8 221.8 %reduce-scatter.23.cloned.1.call-start = ((), (), s32[]{:S(2)}) async-start(), calls=%async_computation.22 | async-start | bytes 7864320 | tf_op jit(solution)/shard_map/reduce_scatter | solution.py:25
  1357.0 107.7 %copy-start.30 = (f32[768]{0:T(1024)S(1)}, f32[768]{0:T(1024)}, u32[]{:S(2)}) copy-start(f32[768]{0:T(1024)} %param.14) | copy-start | bytes 9220
  1357.0 107.7 %copy-start.32 = (f32[512]{0:T(512)S(1)}, f32[512]{0:T(512)}, u32[]{:S(2)}) copy-start(f32[512]{0:T(512)} %copy-done.31) | copy-start | bytes 6148
  1359.0 112.4 %copy-start.35 = (f32[768]{0:T(1024)S(1)}, f32[768]{0:T(1024)}, u32[]{:S(2)}) copy-start(f32[768]{0:T(1024)} %get-tuple-element.9) | copy-start | bytes 9220
  (36 other events, 389.7 us)
Sparse Core Ops, SparseCore 0:
  17.5 65.1 all-gather.7
  88.3 42.0 reduce-scatter.8
  168.2 110.7 reduce-scatter.10
  281.1 63.9 all-gather.13
  347.0 62.0 all-gather.9
  411.3 97.9 reduce-scatter.16
  511.6 189.1 reduce-scatter.12
  710.4 103.9 all-gather.15
  816.6 56.7 all-gather.11
  875.5 110.7 reduce-scatter.18
  988.6 111.2 reduce-scatter.14
  1104.8 63.9 all-gather.17
  1173.2 24.7 reduce-scatter.20
  1210.6 27.1 all-gather.19
  1243.0 108.4 all-reduce.3
  1353.6 110.9 reduce-scatter.22
where the time goes:
time: 1520 us
  waiting for transfers between devices  1250 us (82%)
  matrix products  95.8 us (6%)
  blocking collectives  66.9 us (4%)
  other arithmetic  61 us (4%)
  local copies, waits for them, and re-layouts  20.5 us (1%)
    reduce_scatter x4, waiting for transfers between devices, narrow_sum(): return lax.psum_scatter(partial_sum, 'col', scatter_dimension=0, tiled=True)  421 us
    reduce_scatter x4, waiting for transfers between devices, rows_sum(): return lax.psum_scatter(partial_sum, 'row', scatter_dimension=0, tiled=True)  334 us
    all_gather x4, waiting for transfers between devices, widen(): return lax.all_gather(tensor, 'col', axis=0, tiled=True)  237 us
    all_gather x3, waiting for transfers between devices, rows_gather(): return lax.all_gather(tensor, 'row', axis=0, tiled=True)  161 us
    psum x1, waiting for transfers between devices, shards(): lax.psum(grad_w_qkv.astype(jnp.bfloat16), 'batch').astype(jnp.float32)  101 us
    psum x1, blocking collectives, shards(): lax.psum((grad_gain_attn, grad_gain_mlp), ('batch', 'col'))  33 us
  transfers between devices with their start and end apart: 16, of which 16 were waited for; matrix products, arithmetic and copies ran while one was open for 6% of the time, Pallas kernels for 0%

commit v1 on v0

--- a/solution.py
+++ b/solution.py
@@ -261,9 +261,228 @@
     )
 
 
+def swap_row(tensor):
+    return lax.ppermute(tensor, "row", [(0, 1), (1, 0)])
+
+
+def swap_core(tensor):
+    return lax.ppermute(tensor, "batch", [(0, 1), (1, 0), (2, 3), (3, 2)])
+
+
+def swap_chip(tensor):
+    return lax.ppermute(tensor, "batch", [(0, 2), (2, 0), (1, 3), (3, 1)])
+
+
+def pick(tensor, index, axis=0):
+    return lax.dynamic_index_in_dim(tensor, index, axis, keepdims=False)
+
+
+def in_order(mine, other, index, axis=0):
+    first = jnp.where(index == 0, mine, other)
+    second = jnp.where(index == 0, other, mine)
+    return jnp.stack([first, second], axis=axis)
+
+
+def gather_team(tensor):
+    full = lax.all_gather(tensor, ("batch", "row"), axis=0, tiled=False)
+    full = full.reshape(4, 2, *tensor.shape)
+    return jnp.transpose(full, (0, 2, 1, 3))
+
+
+def scatter_team(partial):
+    parts = jnp.transpose(partial, (0, 2, 1, 3)).reshape(8, partial.shape[1], partial.shape[3])
+    return lax.psum_scatter(parts, ("batch", "row"), scatter_dimension=0, tiled=False)
+
+
+def fast_shards(
+    inputs,
+    segments,
+    positions,
+    gain_attn,
+    gain_mlp,
+    w_qkv,
+    w_out,
+    w_gate,
+    w_up,
+    w_down,
+    grad_output,
+):
+    bf = jnp.bfloat16
+    f32 = jnp.float32
+    b = lax.axis_index("batch")
+    y = lax.axis_index("row")
+    z = lax.axis_index("col")
+    c = lax.rem(b, 2)
+    cols = lax.axis_size("col")
+    seq_len = segments.shape[1]
+    tokens, feats = inputs.shape
+    query_cols = w_out.shape[0]
+    block_cols = w_qkv.shape[1]
+    head_size = block_cols - query_cols - (block_cols - query_cols) // 2
+    group_heads = query_cols // head_size
+    score_scale = 1.0 / math.sqrt(head_size)
+    ff_cols = w_gate.shape[1]
+    part = ff_cols // 8
+
+    def eighth(index):
+        return jnp.stack(
+            [
+                lax.dynamic_slice_in_dim(w_gate, index * part, part, 1).T,
+                lax.dynamic_slice_in_dim(w_up, index * part, part, 1).T,
+                lax.dynamic_slice_in_dim(w_down, index * part, part, 0),
+            ]
+        )
+
+    mine_w = eighth(2 * b + y)
+    their_w = swap_row(eighth(2 * b + 1 - y))
+    full_w = jnp.concatenate(
+        [jnp.where(y == 0, mine_w, their_w), jnp.where(y == 0, their_w, mine_w)], axis=2
+    )
+    gate_up_w = lax.all_gather(full_w[:2], "col", axis=1, tiled=True)
+    down_w = lax.all_gather(full_w[2], "col", axis=0, tiled=True)
+    gate_w, up_w = gate_up_w[0], gate_up_w[1]
+
+    places = jnp.stack([segments, positions])
+    places = in_order(places, swap_row(places), y, axis=1).reshape(2, 4, seq_len)
+    places = pick(places, z, 1)
+    places = in_order(places, swap_core(places), c, axis=1)
+    seg, pos = places[0], places[1]
+    cosine_table, sine_table = rope_tables(pos, head_size)
+
+    wa = jnp.concatenate([w_qkv, w_out.T], axis=1)
+    wa = lax.all_gather(wa, "col", axis=0, tiled=False)
+    wa = lax.dynamic_slice_in_dim(wa, 2 * c, 2, 0)
+    wa_mine, wa_theirs = pick(wa, y), pick(wa, 1 - y)
+    wq_mine, wo_mine = wa_mine[:, :block_cols], wa_mine[:, block_cols:]
+    wq_theirs, wo_theirs = wa_theirs[:, :block_cols], wa_theirs[:, block_cols:]
+
+    normed_one, inverse_one, hidden_one = norm_forward(inputs, gain_attn)
+    wide_one = in_order(hidden_one, swap_core(hidden_one), c).reshape(2 * tokens, feats)
+    sent = matmul(wide_one, wq_theirs).astype(bf)
+    qkv_local = matmul(wide_one, wq_mine) + swap_row(sent).astype(f32)
+    seq_count = 2
+    queries = qkv_local[:, :query_cols].reshape(seq_count, seq_len, group_heads, head_size)
+    key_part = qkv_local[:, query_cols : query_cols + head_size].reshape(
+        seq_count, seq_len, head_size
+    )
+    value_matrix = (
+        qkv_local[:, query_cols + head_size :].reshape(seq_count, seq_len, head_size).astype(bf)
+    )
+    rotary_queries = rotate(queries, cosine_table[:, :, None, :], sine_table[:, :, None, :]).astype(
+        bf
+    )
+    rotary_keys = rotate(key_part, cosine_table, sine_table).astype(bf)
+    attention_output, log_total = attend_forward(
+        rotary_queries, rotary_keys, value_matrix, seg, score_scale
+    )
+    attended = attention_output.reshape(2 * tokens, query_cols)
+    attended_theirs = swap_row(attended)
+    out_partial = right_t(attended, wo_mine) + right_t(attended_theirs, wo_theirs)
+    out_partial = out_partial.reshape(2, tokens, feats)
+    mixed_in = inputs + (pick(out_partial, c) + swap_core(pick(out_partial, 1 - c)))
+    normed_two, inverse_two, hidden_two = norm_forward(mixed_in, gain_mlp)
+
+    wide_two = gather_team(hidden_two).reshape(4 * tokens, 2 * feats)
+    gate_vals = right_t(wide_two, gate_w)
+    up_vals = right_t(wide_two, up_w)
+    gate_sigmoid = jax.nn.sigmoid(gate_vals)
+    activated = (gate_vals * gate_sigmoid * up_vals).astype(bf)
+    result_partial = matmul(activated, down_w).astype(bf).reshape(4, tokens, 2, feats)
+    result = mixed_in + scatter_team(result_partial).astype(f32)
+
+    wide_grad = gather_team(grad_output.astype(bf)).reshape(4 * tokens, 2 * feats)
+    grad_act = right_t(wide_grad, down_w)
+    grad_w_down = left_t(activated, wide_grad).astype(bf)
+    grad_gate = (
+        grad_act * up_vals * gate_sigmoid * (1.0 + gate_vals * (1.0 - gate_sigmoid))
+    ).astype(bf)
+    grad_up = (grad_act * gate_vals * gate_sigmoid).astype(bf)
+    grad_w_gate = left_t(grad_gate, wide_two).astype(bf)
+    grad_w_up = left_t(grad_up, wide_two).astype(bf)
+    hidden_partial = matmul(grad_gate, gate_w) + matmul(grad_up, up_w)
+    grad_hidden_two = scatter_team(hidden_partial.astype(bf).reshape(4, tokens, 2, feats)).astype(
+        f32
+    )
+    grad_mixed, grad_gain_mlp = norm_backward(
+        grad_output, grad_hidden_two, normed_two, inverse_two, gain_mlp
+    )
+
+    grad_mixed_b = grad_mixed.astype(bf)
+    wide_mixed = in_order(grad_mixed_b, swap_core(grad_mixed_b), c).reshape(2 * tokens, feats)
+    grad_wo_mine = left_t(wide_mixed, attended)
+    grad_wo_theirs = left_t(wide_mixed, attended_theirs)
+    sent = matmul(wide_mixed, wo_theirs).astype(bf)
+    attention_output_gradient = (
+        (matmul(wide_mixed, wo_mine) + swap_row(sent).astype(f32))
+        .astype(bf)
+        .reshape(seq_count, seq_len, group_heads, head_size)
+    )
+    grad_qrot, grad_krot, grad_value = attend_backward(
+        rotary_queries,
+        rotary_keys,
+        value_matrix,
+        seg,
+        log_total,
+        attention_output_gradient,
+        score_scale,
+    )
+    grad_query = rotate(grad_qrot, cosine_table[:, :, None, :], -sine_table[:, :, None, :]).reshape(
+        2 * tokens, query_cols
+    )
+    grad_key = rotate(grad_krot, cosine_table, -sine_table).reshape(2 * tokens, head_size)
+    grad_qkv = jnp.concatenate(
+        [grad_query, grad_key, grad_value.reshape(2 * tokens, head_size)], axis=1
+    ).astype(bf)
+    grad_qkv_theirs = swap_row(grad_qkv)
+    one_partial = right_t(grad_qkv, wq_mine) + right_t(grad_qkv_theirs, wq_theirs)
+    one_partial = one_partial.reshape(2, tokens, feats)
+    grad_hidden_one = pick(one_partial, c) + swap_core(pick(one_partial, 1 - c))
+    grad_inputs, grad_gain_attn = norm_backward(
+        grad_mixed, grad_hidden_one, normed_one, inverse_one, gain_attn
+    )
+    grad_gain_attn, grad_gain_mlp = lax.psum((grad_gain_attn, grad_gain_mlp), ("batch", "col"))
+
+    grad_wq = in_order(left_t(wide_one, grad_qkv), left_t(wide_one, grad_qkv_theirs), y)
+    grad_wo = in_order(grad_wo_mine, grad_wo_theirs, y)
+    grad_wa = jnp.concatenate([grad_wq, grad_wo], axis=2).astype(bf)
+    blank = jnp.zeros_like(grad_wa)
+    grad_wa = jnp.concatenate(
+        [jnp.where(c == 0, grad_wa, blank), jnp.where(c == 0, blank, grad_wa)], axis=0
+    )
+    grad_wa = lax.psum_scatter(grad_wa, "col", scatter_dimension=0, tiled=False)
+    grad_wa = lax.psum(grad_wa, "batch").astype(f32)
+    grad_w_qkv = grad_wa[:, :block_cols]
+    grad_w_out = grad_wa[:, block_cols:].T
+
+    def assemble(stacked):
+        summed = lax.psum_scatter(stacked, "col", scatter_dimension=1, tiled=True)
+        halves = summed.reshape(-1, part, 2, feats)
+        mine, theirs = pick(halves, y, 2), pick(halves, 1 - y, 2)
+        pair = in_order(mine, swap_row(theirs), y, axis=1)
+        return lax.all_gather(pair, "batch", axis=1, tiled=False).reshape(-1, ff_cols, feats)
+
+    grad_w_down = assemble(grad_w_down[None])[0].astype(f32)
+    grads = assemble(jnp.stack([grad_w_gate, grad_w_up]))
+    grad_w_gate = grads[0].T.astype(f32)
+    grad_w_up = grads[1].T.astype(f32)
+    return (
+        result,
+        grad_inputs,
+        grad_gain_attn,
+        grad_gain_mlp,
+        grad_w_qkv,
+        grad_w_out,
+        grad_w_gate,
+        grad_w_up,
+        grad_w_down,
+    )
+
+
 def solution(mesh):
+    shape = mesh.shape
+    team = shape["batch"] == 4 and shape["row"] == 2 and shape["col"] == 4
     return jax.shard_map(
-        shards,
+        fast_shards if team else shards,
         mesh=mesh,
         in_specs=(
             P(("batch", "col"), "row"),

time: 1520 us -> 745 us (0.49)
  waiting for transfers between devices: 1250 us -> 388 us
  local copies, waits for them, and re-layouts: 20.5 us -> 123 us
    reduce_scatter x8 -> x5, waiting for transfers between devices: 754 us -> 129 us  [the longest x2 77.1 us: scatter_team(): lax.psum_scatter(parts, ('batch', 'row'), scatter_dimension=0, tiled=False)]
    all_gather x7, waiting for transfers between devices: 398 us -> 158 us  [the longest x1 61.1 us: fast_shards(): wa = lax.all_gather(wa, 'col', axis=0, tiled=False)]
    ppermute x0 -> x13, waiting for transfers between devices: none -> 68 us  [the longest x8 65.1 us: swap_row(): return lax.ppermute(tensor, 'row', [(0, 1), (1, 0)])]
    psum x1, waiting for transfers between devices: 101 us -> 33.2 us  [fast_shards(): grad_wa = lax.psum(grad_wa, 'batch').astype(f32)]
    reshape x4 -> x11, local copies, waits for them, and re-layouts: 2.22 us -> 60 us  [the longest x2 23.7 us: gather_team(): full = full.reshape(4, 2, *tensor.shape)]
    dot_general x5 -> x7, matrix products: 30.4 us -> 32 us  [right_t(): jnp.einsum('tb,ab->ta', left, right, preferred_element_type=jnp.float32)]
  transfers between devices with their start and end apart: 16 -> 26, of which waited for: 16 -> 15; matrix products, arithmetic and copies ran while one was open for 6% -> 30% of each run, Pallas kernels for 0% -> 0%
where the time goes in v1:
time: 745 us; the launch traced here: 734 us
  waiting for transfers between devices  388 us (52%)
  local copies, waits for them, and re-layouts  123 us (17%)
  matrix products  91.1 us (12%)
  blocking collectives  55.9 us (8%)
  other arithmetic  47.7 us (6%)
  between operations  15.6 us (2%)
  starting transfers between devices  12.8 us (2%)
    reduce_scatter x2, waiting for transfers between devices, scatter_team(): lax.psum_scatter(parts, ('batch', 'row'), scatter_dimension=0, tiled=False)  77.1 us
    ppermute x8, waiting for transfers between devices, swap_row(): return lax.ppermute(tensor, 'row', [(0, 1), (1, 0)])  65.1 us
    all_gather x1, waiting for transfers between devices, fast_shards(): wa = lax.all_gather(wa, 'col', axis=0, tiled=False)  61.1 us
    reduce_scatter x2, waiting for transfers between devices, assemble(): summed = lax.psum_scatter(stacked, 'col', scatter_dimension=1, tiled=True)  52.1 us
    all_gather x1, waiting for transfers between devices, fast_shards(): gate_up_w = lax.all_gather(full_w[:2], 'col', axis=1, tiled=True)  49.6 us
    all_gather x2, waiting for transfers between devices, gather_team(): full = lax.all_gather(tensor, ('batch', 'row'), axis=0, tiled=False)  37.8 us
    psum x1, blocking collectives, fast_shards(): lax.psum((grad_gain_attn, grad_gain_mlp), ('batch', 'col'))  35.4 us
    psum x1, waiting for transfers between devices, fast_shards(): grad_wa = lax.psum(grad_wa, 'batch').astype(f32)  33.2 us
  transfers between devices with their start and end apart: 26, of which 15 were waited for; matrix products, arithmetic and copies ran while one was open for 30% of the time, Pallas kernels for 0%

profile of v1, /device:TPU:0, one launch (start us, length us, event | category | flops | bytes accessed | tf_op | source)
XLA Modules:
  0.0 734.5 jit_solution(1775398655086487406)
XLA Ops:
  28.8 61.1 %all-gather.16.cloned.1.call-done = bf16[3072,576]{1,0:T(8,128)(2,1)} async-done(((bf16[768,576]{1,0:T(8,128)(2,1)}), bf16[3072,576]{1,0:T(8,128)(2,1)}) %all-gather.16.cloned.1.call-update) | async-done | bytes 3538960 | tf_op jit(solution)/shard_map/all_gather | solution.py:353
  97.3 24.2 %collective-permute-done.1 = bf16[1024,384]{0,1:T(8,128)(2,1)} collective-permute-done((bf16[1024,384]{0,1:T(8,128)(2,1)}, bf16[1024,384]{0,1:T(8,128)(2,1)}, u32[]{:S(2)}, u32[]{:S(2)}) %collective-permute-start.1) | collective-permute-done | bytes 786464 | tf_op jit(solution)/shard_map/ppermute | solution.py:265
  142.0 9.4 %collective-permute-done.4 = bf16[1024,192]{0,1:T(8,128)(2,1)S(1)} collective-permute-done((bf16[1024,192]{0,1:T(8,128)(2,1)S(1)}, bf16[1024,192]{0,1:T(8,128)(2,1)S(1)}, u32[]{:S(2)}, u32[]{:S(2)}) %collective-permute-start.4) | collective-permute-done | bytes 393248 | tf_op jit(solution)/shard_map/ppermute | solution.py:265
  169.6 11.9 %copy.93 = bf16[4,2,512,768]{3,1,2,0:T(2,128)(2,1)S(1)} copy(bf16[4,2,512,768]{3,2,1,0:T(8,128)(2,1)} %bitcast.288) | data formatting | bytes 12582912 | tf_op jit(solution)/shard_map/reshape | solution.py:288
  185.5 9.0 %all-gather.20.cloned.1.call-done = bf16[1,512,1536]{2,1,0:T(8,128)(2,1)} async-done(((bf16[1,128,1536]{2,1,0:T(8,128)(2,1)}), bf16[1,512,1536]{2,1,0:T(8,128)(2,1)}) %all-gather.20.cloned.1.call-update) | async-done | bytes 1572880 | tf_op jit(solution)/shard_map/all_gather | solution.py:342
  194.5 8.8 %fusion.19 = f32[512,2048]{0,1:T(8,128)} fusion(bf16[2048,1536]{1,0:T(8,128)(2,1)} %bitcast.294, bf16[1,512,1536]{2,1,0:T(8,128)(2,1)} %all-gather.20.cloned.1.call-done), kind=kOutput, calls=%fused_computation.52 | convolution fusion | flops 3221225472 | bytes 12058624 | tf_op jit(solution)/shard_map/tb,ab->ta/dot_general | solution.py:144
  203.3 37.8 %all-gather.18.cloned.1.call-done = bf16[4096,768]{1,0:T(8,128)(2,1)} async-done(((bf16[512,768]{1,0:T(8,128)(2,1)}), bf16[4096,768]{1,0:T(8,128)(2,1)}) %all-gather.18.cloned.1.call-update) | async-done | bytes 6291472 | tf_op jit(solution)/shard_map/all_gather | solution.py:287
  241.1 11.9 %copy.87 = bf16[4,2,512,768]{3,1,2,0:T(2,128)(2,1)S(1)} copy(bf16[4,2,512,768]{3,2,1,0:T(8,128)(2,1)} %bitcast.293) | data formatting | bytes 12582912 | tf_op jit(solution)/shard_map/reshape | solution.py:288
  256.9 49.6 %all-gather.14.cloned.1.call-done = bf16[2,512,1536]{2,1,0:T(8,128)(2,1)} async-done(((bf16[2,128,1536]{2,1,0:T(8,128)(2,1)}), bf16[2,512,1536]{2,1,0:T(8,128)(2,1)}) %all-gather.14.cloned.1.call-update) | async-done | bytes 3145744 | tf_op jit(solution)/shard_map/all_gather | solution.py:341
  306.6 8.8 %fusion.25 = f32[2048,512]{1,0:T(8,128)} fusion(bf16[2048,1536]{1,0:T(8,128)(2,1)} %bitcast.289, bf16[2,512,1536]{2,1,0:T(8,128)(2,1)} %all-gather.14.cloned.1.call-done), kind=kOutput, calls=%fused_computation.70 | convolution fusion | flops 3221225472 | bytes 12058624 | tf_op jit(solution)/shard_map/tb,ab->ta/dot_general | solution.py:144
  315.4 8.8 %fusion.7 = (bf16[2048,512]{1,0:T(8,128)(2,1)}, bf16[2048,512]{1,0:T(8,128)(2,1)}, bf16[2048,512]{1,0:T(8,128)(2,1)S(1)}) fusion(f32[512,2048]{0,1:T(8,128)S(1)} %copy-done.65, f32[2048,512]{1,0:T(8,128)} %fusion.25, bf16[2048,1536]{1,0:T(8,128)(2,1)S(1)} %bitcast.292, bf16[2,512,1536]{2,1,0:T(8,128)(2,1)S(1)} %copy-done.60), kind=kOutput, calls=%fused_computation.13 | convolution fusion | flops 3238002688 | bytes 22544384 | tf_op jit(solution)/shard_map/tb,ab->ta/dot_general | solution.py:144
  335.8 7.0 add_convert_fusion
  342.8 13.6 %reshape.165 = bf16[4,512,2,768]{3,2,1,0:T(2,128)(2,1)} reshape(bf16[2048,1536]{1,0:T(8,128)(2,1)} %add_convert_fusion) | data formatting | bytes 12582912 | tf_op jit(solution)/shard_map/reshape | solution.py:403
  356.4 6.4 copy.95
  363.0 7.1 fusion.10
  370.1 6.8 fusion.9
  388.2 40.2 %reduce-scatter.8.cloned.1.call-done = bf16[1,512,768]{2,1,0:T(8,128)(2,1)} async-done(((bf16[8,512,768]{2,1,0:T(8,128)(2,1)}), bf16[1,512,768]{2,1,0:T(8,128)(2,1)}) %reduce-scatter.8.cloned.1.call-update) | async-done | bytes 786448 | tf_op jit(solution)/shard_map/reduce_scatter | solution.py:294
  439.6 52.1 %reduce-scatter.12.cloned.1.call-done = bf16[2,128,1536]{2,1,0:T(8,128)(2,1)} async-done(((bf16[2,512,1536]{2,1,0:T(8,128)(2,1)}), bf16[2,128,1536]{2,1,0:T(8,128)(2,1)}) %reduce-scatter.12.cloned.1.call-update) | async-done | bytes 786448 | tf_op jit(solution)/shard_map/reduce_scatter | solution.py:458
  532.5 15.2 %collective-permute-done.9 = bf16[1024,384]{0,1:T(8,128)(2,1)S(1)} collective-permute-done((bf16[1024,384]{0,1:T(8,128)(2,1)S(1)}, bf16[1024,384]{0,1:T(8,128)(2,1)S(1)}, u32[]{:S(2)}, u32[]{:S(2)}) %collective-permute-start.9) | collective-permute-done | bytes 786464 | tf_op jit(solution)/shard_map/ppermute | solution.py:265
  554.1 6.9 convolution_convert_fusion
  561.0 13.6 %reshape.161 = bf16[4,512,2,768]{3,2,1,0:T(2,128)(2,1)} reshape(bf16[2048,1536]{1,0:T(8,128)(2,1)} %convolution_convert_fusion) | data formatting | bytes 12582912 | tf_op jit(solution)/shard_map/reshape | solution.py:390
  608.7 35.4 %all-reduce = (f32[768]{0:T(1024)}, f32[768]{0:T(1024)}) all-reduce(f32[768]{0:T(1024)S(1)} %get-tuple-element.36, f32[768]{0:T(1024)S(1)} %copy-done.55), channel_id=1, replica_groups=mesh['batch'=4,'row'=2,'col'=4] {'batch','col'}, use_global_device_ids=true, to_apply=%region_14.15 | all-reduce | flops 1536 | bytes 12288 | tf_op jit(solution)/shard_map/psum | solution.py:443
  649.0 36.9 %reduce-scatter.6.cloned.1.call-done = bf16[1,512,768]{2,1,0:T(8,128)(2,1)} async-done(((bf16[8,512,768]{2,1,0:T(8,128)(2,1)}), bf16[1,512,768]{2,1,0:T(8,128)(2,1)}) %reduce-scatter.6.cloned.1.call-update) | async-done | bytes 786448 | tf_op jit(solution)/shard_map/reduce_scatter | solution.py:294
  690.7 33.2 %all-reduce.3.cloned.1.call-done = bf16[768,576]{0,1:T(8,128)(2,1)} async-done(((bf16[768,576]{0,1:T(8,128)(2,1)}), bf16[768,576]{0,1:T(8,128)(2,1)}) %all-reduce.3.cloned.1.call-update) | async-done | bytes 884752 | tf_op jit(solution)/shard_map/psum | solution.py:453
  (312 shorter events, 203.5 us)
Async XLA Ops:
  7.2 82.7 %all-gather.16.cloned.1.call-start = ((), (), s32[]{:S(2)}) async-start(), calls=%async_computation.12 | async-start | bytes 4915200 | tf_op jit(solution)/shard_map/all_gather | solution.py:353
  10.6 159.0 %all-gather.22.cloned.1.call-start = ((), (), s32[]{:S(2)}) async-start(), calls=%async_computation.15 | async-start | bytes 7077888 | tf_op jit(solution)/shard_map/all_gather | solution.py:287
  11.7 182.8 %all-gather.20.cloned.1.call-start = ((), (), s32[]{:S(2)}) async-start(), calls=%async_computation.14 | async-start | bytes 1966080 | tf_op jit(solution)/shard_map/all_gather | solution.py:342
  11.8 14.2 %collective-permute-start.2 = (s32[2,2,512]{2,1,0:T(2,128)S(1)}, s32[2,2,512]{2,1,0:T(2,128)S(1)}, u32[]{:S(2)}, u32[]{:S(2)}) collective-permute-start(s32[2,2,512]{2,1,0:T(2,128)S(1)} %pad_add_fusion.1), channel_id=1, source_target_pairs={{0,4},{4,0},{1,5},{5,1},{2,6},{6,2},{3,7},{7,3},{8,12},{12,8},{9,1... | collective-permute-start | bytes 24584 | tf_op jit(solution)/shard_map/ppermute | solution.py:265
  20.2 5.9 collective-permute-start
  25.4 114.8 %collective-permute-start.6 = (bf16[3,128,768]{2,1,0:T(8,128)(2,1)}, bf16[3,128,768]{2,1,0:T(8,128)(2,1)}, u32[]{:S(2)}, u32[]{:S(2)}) collective-permute-start(bf16[3,128,768]{2,1,0:T(8,128)(2,1)} %pad_maximum_fusion.7), channel_id=1, source_target_pairs={{0,4},{4,0},{1,5},{5,1},{2,6},{6,2},{3,7},{7,3},{8,12},{12,8},{9,1... | collective-permute-start | bytes 1769480 | tf_op jit(solution)/shard_map/ppermute | solution.py:265
  93.6 27.9 %collective-permute-start.1 = (bf16[1024,384]{0,1:T(8,128)(2,1)}, bf16[1024,384]{0,1:T(8,128)(2,1)}, u32[]{:S(2)}, u32[]{:S(2)}) collective-permute-start(bf16[1024,384]{0,1:T(8,128)(2,1)} %convolution_convert_fusion.4), channel_id=1, source_target_pairs={{0,4},{4,0},{1,5},{5,1},{2,6},{6,2},{3,7},{7,3},{8,12},{12,8},{9,1... | collective-permute-start | bytes 2359304 | tf_op jit(solution)/shard_map/ppermute | solution.py:265
  138.6 12.8 %collective-permute-start.4 = (bf16[1024,192]{0,1:T(8,128)(2,1)S(1)}, bf16[1024,192]{0,1:T(8,128)(2,1)S(1)}, u32[]{:S(2)}, u32[]{:S(2)}) collective-permute-start(bf16[1024,192]{0,1:T(8,128)(2,1)S(1)} %bitcast.302), channel_id=1, source_target_pairs={{0,4},{4,0},{1,5},{5,1},{2,6},{6,2},{3,7},{7,3},{8,12},{12,8},{9,1... | collective-permute-start | bytes 1179656 | tf_op jit(solution)/shard_map/ppermute | solution.py:265
  157.2 83.9 %all-gather.18.cloned.1.call-start = ((), (), s32[]{:S(2)}) async-start(), calls=%async_computation.13 | async-start | bytes 7077888 | tf_op jit(solution)/shard_map/all_gather | solution.py:287
  168.5 138.1 %all-gather.14.cloned.1.call-start = ((), (), s32[]{:S(2)}) async-start(), calls=%async_computation.5 | async-start | bytes 3932160 | tf_op jit(solution)/shard_map/all_gather | solution.py:341
  169.5 209.5 %reduce-scatter.14.cloned.1.call-start = ((), (), s32[]{:S(2)}) async-start(), calls=%async_computation.11 | async-start | bytes 1966080 | tf_op jit(solution)/shard_map/reduce_scatter | solution.py:458
  330.1 98.2 %reduce-scatter.8.cloned.1.call-start = ((), (), s32[]{:S(2)}) async-start(), calls=%async_computation.7 | async-start | bytes 7077888 | tf_op jit(solution)/shard_map/reduce_scatter | solution.py:294
  362.8 128.9 %reduce-scatter.12.cloned.1.call-start = ((), (), s32[]{:S(2)}) async-start(), calls=%async_computation.10 | async-start | bytes 3932160 | tf_op jit(solution)/shard_map/reduce_scatter | solution.py:458
  378.9 209.4 %all-gather.26.cloned.1.call-start = ((), (), s32[]{:S(2)}) async-start(), calls=%async_computation.17 | async-start | bytes 1966080 | tf_op jit(solution)/shard_map/all_gather | solution.py:462
  381.0 6.3 collective-permute-start.12
  388.1 203.5 %all-gather.24.cloned.1.call-start = ((), (), s32[]{:S(2)}) async-start(), calls=%async_computation.16 | async-start | bytes 3932160 | tf_op jit(solution)/shard_map/all_gather | solution.py:462
  439.6 57.5 %collective-permute-start.7 = (bf16[512,768]{1,0:T(8,128)(2,1)}, bf16[512,768]{1,0:T(8,128)(2,1)}, u32[]{:S(2)}, u32[]{:S(2)}) collective-permute-start(bf16[512,768]{1,0:T(8,128)(2,1)} %fusion.83), channel_id=1, source_target_pairs={{0,8},{8,0},{16,24},{24,16},{1,9},{9,1},{17,25},{25,17},{2,10},{10... | collective-permute-start | bytes 2359304 | tf_op jit(solution)/shard_map/ppermute | solution.py:269
  495.6 12.1 %collective-permute-start.11 = (bf16[2,128,768]{2,1,0:T(8,128)(2,1)S(1)}, bf16[2,128,768]{2,1,0:T(8,128)(2,1)S(1)}, u32[]{:S(2)}, u32[]{:S(2)}) collective-permute-start(bf16[2,128,768]{2,1,0:T(8,128)(2,1)S(1)} %bitcast.320), channel_id=1, source_target_pairs={{0,4},{4,0},{1,5},{5,1},{2,6},{6,2},{3,7},{7,3},{8,12},{12,8},{9,1... | collective-permute-start | bytes 1179656 | tf_op jit(solution)/shard_map/ppermute | solution.py:265
  501.2 13.5 %collective-permute-start.8 = (bf16[1024,192]{0,1:T(8,128)(2,1)}, bf16[1024,192]{0,1:T(8,128)(2,1)}, u32[]{:S(2)}, u32[]{:S(2)}) collective-permute-start(bf16[1024,192]{0,1:T(8,128)(2,1)} %convolution_convert_fusion.5), channel_id=1, source_target_pairs={{0,4},{4,0},{1,5},{5,1},{2,6},{6,2},{3,7},{7,3},{8,12},{12,8},{9,1... | collective-permute-start | bytes 1179656 | tf_op jit(solution)/shard_map/ppermute | solution.py:265
  508.7 140.3 %reduce-scatter.10.cloned.1.call-start = ((), (), s32[]{:S(2)}) async-start(), calls=%async_computation.8 | async-start | bytes 4423680 | tf_op jit(solution)/shard_map/reduce_scatter | solution.py:452
  530.3 17.4 %collective-permute-start.9 = (bf16[1024,384]{0,1:T(8,128)(2,1)S(1)}, bf16[1024,384]{0,1:T(8,128)(2,1)S(1)}, u32[]{:S(2)}, u32[]{:S(2)}) collective-permute-start(bf16[1024,384]{0,1:T(8,128)(2,1)S(1)} %constant_dynamic-update-slice_fusion), channel_id=1, source_target_pairs={{0,4},{4,0},{1,5},{5,1},{2,6},{6,2},{3,7},{7,3},{8,12},{12,8},{9,1... | collective-permute-start | bytes 2359304 | tf_op jit(solution)/shard_map/ppermute | solution.py:265
  552.7 133.2 %reduce-scatter.6.cloned.1.call-start = ((), (), s32[]{:S(2)}) async-start(), calls=%async_computation.6 | async-start | bytes 7077888 | tf_op jit(solution)/shard_map/reduce_scatter | solution.py:294
  580.9 143.0 %all-reduce.3.cloned.1.call-start = ((), (), s32[]{:S(2)}) async-start(), calls=%async_computation.9 | async-start | bytes 1769472 | tf_op jit(solution)/shard_map/psum | solution.py:453
  588.3 16.8 %collective-permute-start.10 = (f32[512,768]{1,0:T(8,128)}, f32[512,768]{1,0:T(8,128)}, u32[]{:S(2)}, u32[]{:S(2)}) collective-permute-start(f32[512,768]{1,0:T(8,128)} %dynamic-slice_bitcast_fusion), channel_id=1, source_target_pairs={{0,8},{8,0},{16,24},{24,16},{1,9},{9,1},{17,25},{25,17},{2,10},{10... | collective-permute-start | bytes 4718600 | tf_op jit(solution)/shard_map/ppermute | solution.py:269
  (70 other events, 579.9 us)
Sparse Core Ops, SparseCore 0:
  10.7 79.1 all-gather.15
  92.4 54.8 all-gather.21
  157.3 37.1 all-gather.19
  196.8 44.2 all-gather.17
  243.1 63.4 all-gather.13
  330.3 34.0 reduce-scatter.13
  367.8 60.5 reduce-scatter.7
  431.3 60.3 reduce-scatter.11
  493.3 19.5 all-gather.25
  514.8 28.4 all-gather.23
  552.8 67.5 reduce-scatter.9
  623.6 62.2 reduce-scatter.5
  688.3 35.5 all-reduce.2

commit v2 on v1

--- a/solution.py
+++ b/solution.py
@@ -1,8 +1,11 @@
+import functools
 import math
 
 import jax
 import jax.numpy as jnp
 from jax import lax
+from jax.experimental import pallas as pl
+from jax.experimental.pallas import tpu as pltpu
 from jax.sharding import PartitionSpec as P
 
 D = 1536
@@ -261,6 +264,641 @@
     )
 
 
+MESH = pl.DeviceIdType.MESH
+
+
+def place(b, y, z):
+    return {"batch": b, "row": y, "col": z}
+
+
+def me():
+    return lax.axis_index("batch"), lax.axis_index("row"), lax.axis_index("col")
+
+
+def greet(partners):
+    barrier = pltpu.get_barrier_semaphore()
+    for partner in partners:
+        pl.semaphore_signal(barrier, inc=1, device_id=partner, device_id_type=MESH)
+    pl.semaphore_wait(barrier, len(partners))
+
+
+def send(src, dst, send_sem, recv_sem, target):
+    copy = pltpu.make_async_remote_copy(
+        src_ref=src,
+        dst_ref=dst,
+        send_sem=send_sem,
+        recv_sem=recv_sem,
+        device_id=target,
+        device_id_type=MESH,
+    )
+    copy.start()
+    return copy
+
+
+def landed(ref, sem):
+    pltpu.make_async_copy(ref, ref, sem).wait()
+
+
+def xor(index, bit):
+    return index + bit - 2 * bit * lax.rem(lax.div(index, jnp.int32(bit)), 2)
+
+
+def dot_t(left, right):
+    return lax.dot_general(left, right, (((1,), (1,)), ((), ())), preferred_element_type=jnp.float32)
+
+
+OWN, SIB, FAR, FAR_SIB = range(4)
+
+
+def gate_up_kernel(
+    hid, wg, wu, wide, gate, up, act, wide_v, wg_v, wu_v, gate_v, up_v, act_v,
+    own_send, fwd_send, recv, local, out_sem,
+):
+    b, y, z = me()
+    tokens, feats = hid.shape
+    half = tokens // 2
+    near, across, beside = place(xor(b, 1), y, z), place(xor(b, 2), y, z), place(b, 1 - y, z)
+    loads = [
+        pltpu.make_async_copy(hid, wide_v.at[0, OWN], local.at[0]),
+        pltpu.make_async_copy(wg, wg_v, local.at[1]),
+        pltpu.make_async_copy(wu, wu_v, local.at[2]),
+    ]
+    for load in loads:
+        load.start()
+    greet([near, across, beside])
+
+    def rows(h):
+        return pl.ds(h * half, half)
+
+    copies = []
+    for i in (0, 1):
+        for t, (target, yy, bb, h) in enumerate(
+            ((across, 0, FAR, i), (beside, 1, OWN, 1 - i), (near, 0, SIB, i))
+        ):
+            copies.append(
+                send(
+                    hid.at[rows(h)], wide_v.at[yy, bb, rows(h)], own_send.at[t, i], recv.at[yy, bb, h], target
+                )
+            )
+    for load in loads:
+        load.wait()
+
+    def forward(slot, yy, bb, h, target, to_y, to_b):
+        copies.append(
+            send(
+                wide_v.at[yy, bb, rows(h)],
+                wide_v.at[to_y, to_b, rows(h)],
+                fwd_send.at[slot],
+                recv.at[to_y, to_b, h],
+                target,
+            )
+        )
+
+    def arrive(yy, bb, h):
+        landed(wide_v.at[yy, bb, rows(h)], recv.at[yy, bb, h])
+
+    step = 256
+
+    def work(yy, bb, h, first):
+        for w_v, total in ((wg_v, gate_v), (wu_v, up_v)):
+
+            def body(i, _, w_v=w_v, total=total):
+                out = pl.ds(pl.multiple_of(i * step, step), step)
+                value = dot_t(wide_v[yy, bb, rows(h), :], w_v[out, pl.ds(yy * feats, feats)])
+                if first:
+                    total[bb, rows(h), out] = value
+                else:
+                    total[bb, rows(h), out] += value
+                return 0
+
+            lax.fori_loop(0, w_v.shape[0] // step, body, 0)
+
+    def finish(bb, h):
+        chunk = 32
+
+        def body(i, _):
+            r = pl.ds(pl.multiple_of(h * half + i * chunk, chunk), chunk)
+            g = gate_v[bb, r, :]
+            act_v[bb, r, :] = (g * jax.nn.sigmoid(g) * up_v[bb, r, :]).astype(act_v.dtype)
+            return 0
+
+        lax.fori_loop(0, half // chunk, body, 0)
+        for k, (src, dst) in enumerate(((gate_v, gate), (up_v, up), (act_v, act))):
+            pltpu.make_async_copy(src.at[bb, rows(h)], dst.at[bb, rows(h)], out_sem.at[k]).start()
+
+    work(0, OWN, 0, True)
+    work(0, OWN, 1, True)
+    arrive(0, SIB, 0)
+    work(0, SIB, 0, True)
+    arrive(0, SIB, 1)
+    work(0, SIB, 1, True)
+    arrive(0, FAR, 0)
+    forward(0, 0, FAR, 0, near, 0, FAR_SIB)
+    forward(1, 0, FAR, 0, beside, 1, FAR)
+    arrive(1, OWN, 1)
+    forward(2, 1, OWN, 1, near, 1, SIB)
+    forward(3, 1, OWN, 1, across, 1, FAR)
+    work(0, FAR, 0, True)
+    work(1, OWN, 1, False)
+    finish(OWN, 1)
+    arrive(0, FAR_SIB, 0)
+    work(0, FAR_SIB, 0, True)
+    arrive(1, SIB, 1)
+    work(1, SIB, 1, False)
+    finish(SIB, 1)
+    arrive(0, FAR, 1)
+    forward(4, 0, FAR, 1, near, 0, FAR_SIB)
+    arrive(1, OWN, 0)
+    forward(5, 1, OWN, 0, near, 1, SIB)
+    work(0, FAR, 1, True)
+    work(1, OWN, 0, False)
+    finish(OWN, 0)
+    arrive(0, FAR_SIB, 1)
+    work(0, FAR_SIB, 1, True)
+    arrive(1, SIB, 0)
+    work(1, SIB, 0, False)
+    finish(SIB, 0)
+    arrive(1, FAR, 0)
+    forward(6, 1, FAR, 0, near, 1, FAR_SIB)
+    arrive(1, FAR, 1)
+    forward(7, 1, FAR, 1, near, 1, FAR_SIB)
+    work(1, FAR, 0, False)
+    finish(FAR, 0)
+    work(1, FAR, 1, False)
+    finish(FAR, 1)
+    arrive(1, FAR_SIB, 0)
+    arrive(1, FAR_SIB, 1)
+    saves = [
+        pltpu.make_async_copy(wide_v.at[yy], wide.at[:, :, pl.ds(yy * feats, feats)], local.at[yy])
+        for yy in (0, 1)
+    ]
+    for save in saves:
+        save.start()
+    work(1, FAR_SIB, 0, False)
+    finish(FAR_SIB, 0)
+    work(1, FAR_SIB, 1, False)
+    finish(FAR_SIB, 1)
+    for copy in copies:
+        copy.wait_send()
+    for save in saves:
+        save.wait()
+    for k, (src, dst) in enumerate(((gate_v, gate), (up_v, up), (act_v, act))):
+        pltpu.make_async_copy(src, dst, out_sem.at[k]).wait()
+
+
+def gate_up(hidden, gate_w, up_w):
+    tokens, feats = hidden.shape
+    width = gate_w.shape[0]
+    bf, f32 = jnp.bfloat16, jnp.float32
+    any_spec = pl.BlockSpec(memory_space=pl.ANY)
+    dma = pltpu.SemaphoreType.DMA
+    return pl.pallas_call(
+        gate_up_kernel,
+        out_shape=(
+            jax.ShapeDtypeStruct((4, tokens, 2 * feats), bf),
+            jax.ShapeDtypeStruct((4, tokens, width), f32),
+            jax.ShapeDtypeStruct((4, tokens, width), f32),
+            jax.ShapeDtypeStruct((4, tokens, width), bf),
+        ),
+        in_specs=[any_spec] * 3,
+        out_specs=(any_spec,) * 4,
+        scratch_shapes=[
+            pltpu.VMEM((2, 4, tokens, feats), bf),
+            pltpu.VMEM((width, 2 * feats), bf),
+            pltpu.VMEM((width, 2 * feats), bf),
+            pltpu.VMEM((4, tokens, width), f32),
+            pltpu.VMEM((4, tokens, width), f32),
+            pltpu.VMEM((4, tokens, width), bf),
+            dma((3, 2)),
+            dma((8,)),
+            dma((2, 4, 2)),
+            dma((3,)),
+            dma((3,)),
+        ],
+        compiler_params=pltpu.CompilerParams(
+            collective_id=1, has_side_effects=True, vmem_limit_bytes=48 * 2**20
+        ),
+        cost_estimate=pl.CostEstimate(
+            flops=2 * 8 * tokens * feats * 2 * width, bytes_accessed=30 * 2**20, transcendentals=0
+        ),
+        name="gate_up",
+    )(hidden, gate_w, up_w)
+
+
+def team_sum_kernel(pairs, *refs):
+    lefts, rights = refs[:pairs], refs[pairs : 2 * pairs]
+    out = refs[2 * pairs]
+    scratch = refs[2 * pairs + 1 :]
+    lefts_v, rights_v = scratch[:pairs], scratch[pairs : 2 * pairs]
+    (
+        own, near_out, near_in, turn, turn_x, turn_y, far_out, far_in, side_out, side_in,
+        load_sem, near_send, near_recv, turn_send, turn_recv, link_send, link_recv, out_sem,
+    ) = scratch[2 * pairs :]
+    b, y, z = me()
+    tokens, feats = out.shape
+    half = tokens // 2
+    near, across, beside = place(xor(b, 1), y, z), place(xor(b, 2), y, z), place(b, 1 - y, z)
+    loads = []
+    for i in range(pairs):
+        loads.append(pltpu.make_async_copy(rights[i], rights_v[i], load_sem.at[i, 0]))
+        loads.append(pltpu.make_async_copy(lefts[i], lefts_v[i], load_sem.at[i, 1]))
+    for load in loads:
+        load.start()
+    greet([near, across, beside])
+    for load in loads:
+        load.wait()
+
+    def rows(h):
+        return pl.ds(h * half, half)
+
+    step = 256
+
+    def product(bb, yy, store):
+        def body(i, _):
+            r = pl.ds(pl.multiple_of((i // 3) * step, step), step)
+            n = lax.rem(i, 3) * step
+            cols = pl.ds(pl.multiple_of(yy * feats + n, 128), step)
+            value = jnp.dot(lefts_v[0][bb, r, :], rights_v[0][:, cols], preferred_element_type=jnp.float32)
+            for j in range(1, pairs):
+                value += jnp.dot(lefts_v[j][bb, r, :], rights_v[j][:, cols], preferred_element_type=jnp.float32)
+            store(r, pl.ds(pl.multiple_of(n, 128), step), value)
+            return 0
+
+        lax.fori_loop(0, (tokens // step) * (feats // step), body, 0)
+
+    copies = []
+    order = ((FAR, FAR_SIB, 1), (FAR, FAR_SIB, 0), (OWN, SIB, 1), (OWN, SIB, 0))
+    for k, (mine, theirs, yy) in enumerate(order):
+
+        def keep_near(r, cols, value, k=k):
+            near_out[k, r, cols] = value.astype(near_out.dtype)
+
+        def keep_own(r, cols, value, k=k):
+            own[k, r, cols] = value
+
+        product(theirs, yy, keep_near)
+        copies.append(send(near_out.at[k], near_in.at[k], near_send.at[k], near_recv.at[k], near))
+        product(mine, yy, keep_own)
+        if k == 0:
+            landed(near_in.at[0], near_recv.at[0])
+            add_rows(turn, own, near_in, 0, 0, tokens)
+            copies.append(send(turn.at[rows(0)], turn_x, turn_send.at[0], turn_recv.at[0], across))
+            copies.append(send(turn.at[rows(1)], turn_y, turn_send.at[1], turn_recv.at[1], beside))
+        if k == 1:
+            landed(near_in.at[1], near_recv.at[1])
+            add_rows(far_out, own, near_in, 1, 0, half)
+            copies.append(send(far_out.at[rows(0)], far_in.at[rows(0)], link_send.at[0], link_recv.at[0], across))
+        if k == 2:
+            landed(near_in.at[2], near_recv.at[2])
+            add_rows(side_out, own, near_in, 2, half, half)
+            copies.append(send(side_out.at[rows(1)], side_in.at[rows(1)], link_send.at[1], link_recv.at[1], beside))
+    landed(turn_y, turn_recv.at[1])
+    add_rows(far_out, own, near_in, 1, half, half, turn_y, half)
+    copies.append(send(far_out.at[rows(1)], far_in.at[rows(1)], link_send.at[2], link_recv.at[2], across))
+    landed(turn_x, turn_recv.at[0])
+    add_rows(side_out, own, near_in, 2, 0, half, turn_x, 0)
+    copies.append(send(side_out.at[rows(0)], side_in.at[rows(0)], link_send.at[3], link_recv.at[3], beside))
+    landed(near_in.at[3], near_recv.at[3])
+    landed(far_in.at[rows(0)], link_recv.at[0])
+    landed(side_in.at[rows(1)], link_recv.at[1])
+    landed(far_in.at[rows(1)], link_recv.at[2])
+    landed(side_in.at[rows(0)], link_recv.at[3])
+    chunk = 64
+
+    def body(i, _):
+        r = pl.ds(pl.multiple_of(i * chunk, chunk), chunk)
+        f32 = jnp.float32
+        own[3, r, :] = (
+            own[3, r, :]
+            + near_in[3, r, :].astype(f32)
+            + (far_in[r, :].astype(f32) + side_in[r, :].astype(f32))
+        )
+        return 0
+
+    lax.fori_loop(0, tokens // chunk, body, 0)
+    save = pltpu.make_async_copy(own.at[3], out, out_sem)
+    save.start()
+    for copy in copies:
+        copy.wait_send()
+    save.wait()
+
+
+def add_rows(dst, own, near_in, k, start, count, extra=None, extra_start=0):
+    chunk = 64
+
+    def body(i, _):
+        at = start + i * chunk
+        r = pl.ds(pl.multiple_of(at, chunk), chunk)
+        value = own[k, r, :] + near_in[k, r, :].astype(jnp.float32)
+        if extra is not None:
+            value += extra[pl.ds(pl.multiple_of(at - extra_start, chunk), chunk), :].astype(jnp.float32)
+        dst[r, :] = value.astype(dst.dtype)
+        return 0
+
+    lax.fori_loop(0, count // chunk, body, 0)
+
+
+def team_sum(lefts, rights, collective_id):
+    pairs = len(lefts)
+    _, tokens, inner = lefts[0].shape
+    feats = rights[0].shape[1] // 2
+    bf, f32 = jnp.bfloat16, jnp.float32
+    any_spec = pl.BlockSpec(memory_space=pl.ANY)
+    half = tokens // 2
+    return pl.pallas_call(
+        functools.partial(team_sum_kernel, pairs),
+        out_shape=jax.ShapeDtypeStruct((tokens, feats), f32),
+        in_specs=[any_spec] * (2 * pairs),
+        out_specs=any_spec,
+        scratch_shapes=[pltpu.VMEM((4, tokens, inner), bf)] * pairs
+        + [pltpu.VMEM((inner, 2 * feats), bf)] * pairs
+        + [
+            pltpu.VMEM((4, tokens, feats), f32),
+            pltpu.VMEM((4, tokens, feats), bf),
+            pltpu.VMEM((4, tokens, feats), bf),
+            pltpu.VMEM((tokens, feats), bf),
+            pltpu.VMEM((half, feats), bf),
+            pltpu.VMEM((half, feats), bf),
+            pltpu.VMEM((tokens, feats), bf),
+            pltpu.VMEM((tokens, feats), bf),
+            pltpu.VMEM((tokens, feats), bf),
+            pltpu.VMEM((tokens, feats), bf),
+            pltpu.SemaphoreType.DMA((pairs, 2)),
+            pltpu.SemaphoreType.DMA((4,)),
+            pltpu.SemaphoreType.DMA((4,)),
+            pltpu.SemaphoreType.DMA((2,)),
+            pltpu.SemaphoreType.DMA((2,)),
+            pltpu.SemaphoreType.DMA((4,)),
+            pltpu.SemaphoreType.DMA((4,)),
+            pltpu.SemaphoreType.DMA,
+        ],
+        compiler_params=pltpu.CompilerParams(
+            collective_id=collective_id, has_side_effects=True, vmem_limit_bytes=48 * 2**20
+        ),
+        cost_estimate=pl.CostEstimate(
+            flops=2 * 8 * tokens * feats * inner * pairs, bytes_accessed=30 * 2**20, transcendentals=0
+        ),
+        name="team_sum%d" % pairs,
+    )(*lefts, *rights)
+
+
+def weights_kernel(
+    wq, wo, out_q, out_o, held_q, held_o, line_send, line_recv, own_sem, near_send, far_send, recv,
+):
+    b, y, z = me()
+    c = lax.rem(b, 2)
+    sib, far = xor(b, 1), xor(b, 2)
+    far_sib = xor(far, 1)
+    peers = [place(b, y, lax.rem(z + d, 4)) for d in (1, 2, 3)]
+    team = [place(sib, y, z), place(far, y, z), place(far_sib, y, z)]
+    greet(peers + team)
+    rows_q, rows_o = wq.shape[0] // 4, wo.shape[0] // 4
+    mine = (
+        wq.at[pl.ds(pl.multiple_of(b * rows_q, rows_q), rows_q)],
+        wo.at[pl.ds(pl.multiple_of(b * rows_o, rows_o), rows_o)],
+    )
+    held, outs = (held_q, held_o), (out_q, out_o)
+    counts = (rows_q, rows_o)
+    copies = []
+    for w in (0, 1):
+        for d in (0, 2, 1):
+            copies.append(
+                send(mine[w], held[w].at[z], line_send.at[w, d], line_recv.at[w, z], peers[d])
+            )
+        pltpu.make_async_copy(mine[w], held[w].at[z], own_sem.at[w]).start()
+    waits = []
+    for w in (0, 1):
+        for d in (0, 1, 3, 2):
+            block = lax.rem(z + d, 4)
+            src = held[w].at[block]
+            if d == 0:
+                pltpu.make_async_copy(mine[w], src, own_sem.at[w]).wait()
+            else:
+                landed(src, line_recv.at[w, block])
+            owner = lax.div(block, jnp.int32(2))
+            slot = lax.rem(block + y, 2)
+            dst = outs[w].at[slot, pl.ds(pl.multiple_of(b * counts[w], counts[w]), counts[w])]
+            arrival = recv.at[w, slot, b]
+
+            @pl.when(owner == c)
+            def _(src=src, dst=dst, arrival=arrival, w=w, d=d):
+                pltpu.make_async_copy(src, dst, arrival).start()
+                send(src, dst, far_send.at[w, d], arrival, place(far, y, z))
+
+            @pl.when(owner != c)
+            def _(src=src, dst=dst, arrival=arrival, w=w, d=d):
+                send(src, dst, near_send.at[w, d], arrival, place(sib, y, z))
+                send(src, dst, far_send.at[w, d], arrival, place(far_sib, y, z))
+
+            waits.append((w, d, src, owner))
+    for w in (0, 1):
+        for block in (0, 1):
+            for q in range(4):
+                ref = outs[w].at[block, pl.ds(q * counts[w], counts[w])]
+                landed(ref, recv.at[w, block, q])
+    for copy in copies:
+        copy.wait_send()
+    for w, d, src, owner in waits:
+        pltpu.make_async_copy(src, src, far_send.at[w, d]).wait()
+
+        @pl.when(owner != c)
+        def _(src=src, w=w, d=d):
+            pltpu.make_async_copy(src, src, near_send.at[w, d]).wait()
+
+
+def gather_weights(w_qkv, w_out):
+    any_spec = pl.BlockSpec(memory_space=pl.ANY)
+    q, o = w_qkv.shape, w_out.shape
+    dma = pltpu.SemaphoreType.DMA
+    return pl.pallas_call(
+        weights_kernel,
+        out_shape=(
+            jax.ShapeDtypeStruct((2, *q), w_qkv.dtype),
+            jax.ShapeDtypeStruct((2, *o), w_out.dtype),
+        ),
+        in_specs=[any_spec] * 2,
+        out_specs=(any_spec,) * 2,
+        scratch_shapes=[
+            pltpu.VMEM((4, q[0] // 4, q[1]), w_qkv.dtype),
+            pltpu.VMEM((4, o[0] // 4, o[1]), w_out.dtype),
+            dma((2, 3)),
+            dma((2, 4)),
+            dma((2,)),
+            dma((2, 4)),
+            dma((2, 4)),
+            dma((2, 2, 4)),
+        ],
+        compiler_params=pltpu.CompilerParams(
+            collective_id=3, has_side_effects=True, vmem_limit_bytes=8 * 2**20
+        ),
+        cost_estimate=pl.CostEstimate(flops=0, bytes_accessed=10 * 2**20, transcendentals=0),
+        name="gather_weights",
+    )(w_qkv, w_out)
+
+
+def weight_sums_kernel(
+    gq, go, out_q, out_o, got_q, got_o, line_q, line_o, sum_q, sum_o, all_q, all_o, res_q, res_o,
+    part_send, part_recv, line_send, line_recv, all_send, all_recv, out_sem,
+):
+    b, y, z = me()
+    c, x = lax.rem(b, 2), lax.div(b, jnp.int32(2))
+    peers = [place(b, y, lax.rem(z + d, 4)) for d in (1, 2, 3)]
+    team = [place(xor(b, 1), y, z), place(xor(b, 2), y, z), place(xor(xor(b, 2), 1), y, z)]
+    greet(peers + team)
+    f32 = jnp.float32
+    rows = (gq.shape[1] // 4, go.shape[1] // 4)
+    parts, got, line, sums, full, res, outs = (
+        (gq, go), (got_q, got_o), (line_q, line_o), (sum_q, sum_o), (all_q, all_o), (res_q, res_o), (out_q, out_o),
+    )
+    targets = [b, xor(b, 1), xor(b, 2), xor(xor(b, 2), 1)]
+    copies = []
+    for w in (0, 1):
+        for t in (3, 2, 1, 0):
+            q = targets[t]
+            for k in (0, 1):
+                src = parts[w].at[k, pl.ds(pl.multiple_of(q * rows[w], rows[w]), rows[w])]
+                block = 2 * c + (y if k == 0 else 1 - y)
+                dst = got[w].at[block, x]
+                arrival = part_recv.at[w, block, x]
+                if t == 0:
+                    pltpu.make_async_copy(src, dst, arrival).start()
+                else:
+                    copies.append(send(src, dst, part_send.at[w, t, k], arrival, place(q, y, z)))
+    for w in (0, 1):
+        for d in (2, 1, 3, 0):
+            block = lax.rem(z + d, 4)
+            for k in (0, 1):
+                landed(got[w].at[block, k], part_recv.at[w, block, k])
+            total = got[w][block, 0].astype(f32) + got[w][block, 1].astype(f32)
+            if d == 0:
+                res[w][...] = total
+            else:
+                sums[w][d] = total.astype(sums[w].dtype)
+                copies.append(
+                    send(
+                        sums[w].at[d],
+                        line[w].at[z],
+                        line_send.at[w, d],
+                        line_recv.at[w, z],
+                        place(b, y, block),
+                    )
+                )
+    for w in (0, 1):
+        total = res[w][...]
+        for d in (1, 3, 2):
+            block = lax.rem(z + d, 4)
+            landed(line[w].at[block], line_recv.at[w, block])
+            total += line[w][block].astype(f32)
+        full[w][b] = total.astype(full[w].dtype)
+        for t in (3, 2, 1):
+            copies.append(
+                send(
+                    full[w].at[b], full[w].at[b], all_send.at[w, t], all_recv.at[w, b], place(targets[t], y, z)
+                )
+            )
+    for w in (0, 1):
+        for t in (0, 1, 2, 3):
+            q = targets[t]
+            if t > 0:
+                landed(full[w].at[q], all_recv.at[w, q])
+            res[w][...] = full[w][q].astype(f32)
+            save = pltpu.make_async_copy(
+                res[w], outs[w].at[pl.ds(pl.multiple_of(q * rows[w], rows[w]), rows[w])], out_sem
+            )
+            save.start()
+            save.wait()
+    for copy in copies:
+        copy.wait_send()
+
+
+def sum_weights(grad_q, grad_o):
+    any_spec = pl.BlockSpec(memory_space=pl.ANY)
+    bf, f32 = jnp.bfloat16, jnp.float32
+    q = (grad_q.shape[1] // 4, grad_q.shape[2])
+    o = (grad_o.shape[1] // 4, grad_o.shape[2])
+    dma = pltpu.SemaphoreType.DMA
+    return pl.pallas_call(
+        weight_sums_kernel,
+        out_shape=(
+            jax.ShapeDtypeStruct(grad_q.shape[1:], f32),
+            jax.ShapeDtypeStruct(grad_o.shape[1:], f32),
+        ),
+        in_specs=[any_spec] * 2,
+        out_specs=(any_spec,) * 2,
+        scratch_shapes=[
+            pltpu.VMEM((4, 2, *q), bf),
+            pltpu.VMEM((4, 2, *o), bf),
+            pltpu.VMEM((4, *q), bf),
+            pltpu.VMEM((4, *o), bf),
+            pltpu.VMEM((4, *q), bf),
+            pltpu.VMEM((4, *o), bf),
+            pltpu.VMEM((4, *q), bf),
+            pltpu.VMEM((4, *o), bf),
+            pltpu.VMEM(q, f32),
+            pltpu.VMEM(o, f32),
+            dma((2, 4, 2)),
+            dma((2, 4, 2)),
+            dma((2, 4)),
+            dma((2, 4)),
+            dma((2, 4)),
+            dma((2, 4)),
+            dma,
+        ],
+        compiler_params=pltpu.CompilerParams(
+            collective_id=4, has_side_effects=True, vmem_limit_bytes=16 * 2**20
+        ),
+        cost_estimate=pl.CostEstimate(flops=0, bytes_accessed=10 * 2**20, transcendentals=0),
+        name="sum_weights",
+    )(grad_q, grad_o)
+
+
+def gains_kernel(part, out, line, team, total, line_send, line_recv, team_send, team_recv):
+    b, y, z = me()
+    peers = [place(b, y, lax.rem(z + d, 4)) for d in (1, 2, 3)]
+    mates = [place(lax.rem(b + d, 4), y, z) for d in (1, 2, 3)]
+    greet(peers + mates)
+    copies = []
+    for d in range(3):
+        copies.append(send(part, line.at[z], line_send.at[d], line_recv.at[z], peers[d]))
+    line[z] = part[...]
+    for d in (1, 2, 3):
+        block = lax.rem(z + d, 4)
+        landed(line.at[block], line_recv.at[block])
+    value = (line[0] + line[1]) + (line[2] + line[3])
+    total[...] = value
+    team[b] = value
+    for d in range(3):
+        copies.append(send(total, team.at[b], team_send.at[d], team_recv.at[b], mates[d]))
+    for d in (1, 2, 3):
+        mate = lax.rem(b + d, 4)
+        landed(team.at[mate], team_recv.at[mate])
+    out[...] = (team[0] + team[1]) + (team[2] + team[3])
+    for copy in copies:
+        copy.wait_send()
+
+
+def sum_gains(part):
+    spec = pl.BlockSpec(memory_space=pltpu.VMEM)
+    dma = pltpu.SemaphoreType.DMA
+    return pl.pallas_call(
+        gains_kernel,
+        out_shape=jax.ShapeDtypeStruct(part.shape, part.dtype),
+        in_specs=[spec],
+        out_specs=spec,
+        scratch_shapes=[
+            pltpu.VMEM((4, *part.shape), part.dtype),
+            pltpu.VMEM((4, *part.shape), part.dtype),
+            pltpu.VMEM(part.shape, part.dtype),
+            dma((3,)),
+            dma((4,)),
+            dma((3,)),
+            dma((4,)),
+        ],
+        compiler_params=pltpu.CompilerParams(collective_id=5, has_side_effects=True),
+        name="sum_gains",
+    )(part)
+
+
 def swap_row(tensor):
     return lax.ppermute(tensor, "row", [(0, 1), (1, 0)])
 
@@ -273,25 +911,22 @@
     return lax.ppermute(tensor, "batch", [(0, 2), (2, 0), (1, 3), (3, 1)])
 
 
-def pick(tensor, index, axis=0):
-    return lax.dynamic_index_in_dim(tensor, index, axis, keepdims=False)
-
-
-def in_order(mine, other, index, axis=0):
-    first = jnp.where(index == 0, mine, other)
-    second = jnp.where(index == 0, other, mine)
-    return jnp.stack([first, second], axis=axis)
-
-
-def gather_team(tensor):
-    full = lax.all_gather(tensor, ("batch", "row"), axis=0, tiled=False)
-    full = full.reshape(4, 2, *tensor.shape)
-    return jnp.transpose(full, (0, 2, 1, 3))
-
-
-def scatter_team(partial):
-    parts = jnp.transpose(partial, (0, 2, 1, 3)).reshape(8, partial.shape[1], partial.shape[3])
-    return lax.psum_scatter(parts, ("batch", "row"), scatter_dimension=0, tiled=False)
+def both_rows(values):
+    return values + swap_row(values)
+
+
+def fast_norm_forward(values, gain_vec):
+    totals = both_rows(jnp.sum(values * values, axis=1))
+    inverse = lax.rsqrt(totals / D + EPS)[:, None]
+    normed = values * inverse
+    return (normed, inverse, (normed * gain_vec).astype(jnp.bfloat16))
+
+
+def fast_norm_backward(upstream, grad_hidden, normed, inverse, gain_vec):
+    scaled = grad_hidden * gain_vec
+    totals = both_rows(jnp.sum(scaled * normed, axis=1))
+    centre = (totals / D)[:, None]
+    return (upstream + inverse * (scaled - normed * centre), jnp.sum(grad_hidden * normed, axis=0))
 
 
 def fast_shards(
@@ -309,11 +944,7 @@
 ):
     bf = jnp.bfloat16
     f32 = jnp.float32
-    b = lax.axis_index("batch")
-    y = lax.axis_index("row")
-    z = lax.axis_index("col")
-    c = lax.rem(b, 2)
-    cols = lax.axis_size("col")
+    b, y, z = me()
     seq_len = segments.shape[1]
     tokens, feats = inputs.shape
     query_cols = w_out.shape[0]
@@ -325,41 +956,54 @@
     part = ff_cols // 8
 
     def eighth(index):
-        return jnp.stack(
+        gate_up_part = jnp.stack(
             [
                 lax.dynamic_slice_in_dim(w_gate, index * part, part, 1).T,
                 lax.dynamic_slice_in_dim(w_up, index * part, part, 1).T,
-                lax.dynamic_slice_in_dim(w_down, index * part, part, 0),
             ]
         )
-
-    mine_w = eighth(2 * b + y)
-    their_w = swap_row(eighth(2 * b + 1 - y))
-    full_w = jnp.concatenate(
-        [jnp.where(y == 0, mine_w, their_w), jnp.where(y == 0, their_w, mine_w)], axis=2
-    )
-    gate_up_w = lax.all_gather(full_w[:2], "col", axis=1, tiled=True)
-    down_w = lax.all_gather(full_w[2], "col", axis=0, tiled=True)
+        return gate_up_part, lax.dynamic_slice_in_dim(w_down, index * part, part, 0)
+
+    gate_up_mine, down_mine = eighth(2 * b + y)
+    gate_up_sent, down_sent = eighth(2 * b + 1 - y)
+    gate_up_w = jnp.concatenate([gate_up_mine, swap_row(gate_up_sent)], axis=2)
+    down_w = jnp.concatenate([down_mine, swap_row(down_sent)], axis=1)
+    gate_up_w = lax.all_gather(gate_up_w, "col", axis=1, tiled=True)
+    down_w = lax.all_gather(down_w, "col", axis=0, tiled=True)
     gate_w, up_w = gate_up_w[0], gate_up_w[1]
 
-    places = jnp.stack([segments, positions])
-    places = in_order(places, swap_row(places), y, axis=1).reshape(2, 4, seq_len)
-    places = pick(places, z, 1)
-    places = in_order(places, swap_core(places), c, axis=1)
-    seg, pos = places[0], places[1]
+    normed_one, inverse_one, hidden_one = fast_norm_forward(inputs, gain_attn)
+    wq, wo = gather_weights(w_qkv, w_out)
+    wide_one = jnp.concatenate([hidden_one, swap_core(hidden_one)], axis=0)
+
+    grad_b = grad_output.astype(bf)
+    grad_chip, grad_row = swap_chip(grad_b), swap_row(grad_b)
+    grad_corner = swap_chip(grad_row)
+    grad_sibs = swap_core(jnp.stack([grad_b, grad_row, grad_chip, grad_corner]))
+    wide_grad = jnp.concatenate(
+        [
+            jnp.concatenate([grad_b, grad_row], axis=1),
+            jnp.concatenate([grad_sibs[0], grad_sibs[1]], axis=1),
+            jnp.concatenate([grad_chip, grad_corner], axis=1),
+            jnp.concatenate([grad_sibs[2], grad_sibs[3]], axis=1),
+        ],
+        axis=0,
+    )
+
+    places = jnp.stack([segments, positions], axis=1)
+    their_places = swap_row(places)
+    places = jnp.where(
+        y == 0,
+        jnp.concatenate([places, their_places], axis=0),
+        jnp.concatenate([their_places, places], axis=0),
+    )
+    places = lax.dynamic_index_in_dim(places, z, 0, keepdims=False)
+    places = jnp.stack([places, swap_core(places)])
+    seg, pos = places[:, 0], places[:, 1]
     cosine_table, sine_table = rope_tables(pos, head_size)
 
-    wa = jnp.concatenate([w_qkv, w_out.T], axis=1)
-    wa = lax.all_gather(wa, "col", axis=0, tiled=False)
-    wa = lax.dynamic_slice_in_dim(wa, 2 * c, 2, 0)
-    wa_mine, wa_theirs = pick(wa, y), pick(wa, 1 - y)
-    wq_mine, wo_mine = wa_mine[:, :block_cols], wa_mine[:, block_cols:]
-    wq_theirs, wo_theirs = wa_theirs[:, :block_cols], wa_theirs[:, block_cols:]
-
-    normed_one, inverse_one, hidden_one = norm_forward(inputs, gain_attn)
-    wide_one = in_order(hidden_one, swap_core(hidden_one), c).reshape(2 * tokens, feats)
-    sent = matmul(wide_one, wq_theirs).astype(bf)
-    qkv_local = matmul(wide_one, wq_mine) + swap_row(sent).astype(f32)
+    sent = matmul(wide_one, wq[1]).astype(bf)
+    qkv_local = matmul(wide_one, wq[0]) + swap_row(sent).astype(f32)
     seq_count = 2
     queries = qkv_local[:, :query_cols].reshape(seq_count, seq_len, group_heads, head_size)
     key_part = qkv_local[:, query_cols : query_cols + head_size].reshape(
@@ -377,43 +1021,33 @@
     )
     attended = attention_output.reshape(2 * tokens, query_cols)
     attended_theirs = swap_row(attended)
-    out_partial = right_t(attended, wo_mine) + right_t(attended_theirs, wo_theirs)
-    out_partial = out_partial.reshape(2, tokens, feats)
-    mixed_in = inputs + (pick(out_partial, c) + swap_core(pick(out_partial, 1 - c)))
-    normed_two, inverse_two, hidden_two = norm_forward(mixed_in, gain_mlp)
-
-    wide_two = gather_team(hidden_two).reshape(4 * tokens, 2 * feats)
-    gate_vals = right_t(wide_two, gate_w)
-    up_vals = right_t(wide_two, up_w)
+    out_partial = matmul(attended, wo[0]) + matmul(attended_theirs, wo[1])
+    mixed_in = inputs + (out_partial[:tokens] + swap_core(out_partial[tokens:]))
+    normed_two, inverse_two, hidden_two = fast_norm_forward(mixed_in, gain_mlp)
+
+    wide_two, gate_vals, up_vals, activated = gate_up(hidden_two, gate_w, up_w)
+    wide_two = wide_two.reshape(4 * tokens, 2 * feats)
+    flat_act = activated.reshape(4 * tokens, 4 * part)
+
+    grad_w_down = left_t(flat_act, wide_grad).astype(bf)
+    grad_act = right_t(wide_grad, down_w).reshape(gate_vals.shape)
     gate_sigmoid = jax.nn.sigmoid(gate_vals)
-    activated = (gate_vals * gate_sigmoid * up_vals).astype(bf)
-    result_partial = matmul(activated, down_w).astype(bf).reshape(4, tokens, 2, feats)
-    result = mixed_in + scatter_team(result_partial).astype(f32)
-
-    wide_grad = gather_team(grad_output.astype(bf)).reshape(4 * tokens, 2 * feats)
-    grad_act = right_t(wide_grad, down_w)
-    grad_w_down = left_t(activated, wide_grad).astype(bf)
     grad_gate = (
         grad_act * up_vals * gate_sigmoid * (1.0 + gate_vals * (1.0 - gate_sigmoid))
     ).astype(bf)
     grad_up = (grad_act * gate_vals * gate_sigmoid).astype(bf)
-    grad_w_gate = left_t(grad_gate, wide_two).astype(bf)
-    grad_w_up = left_t(grad_up, wide_two).astype(bf)
-    hidden_partial = matmul(grad_gate, gate_w) + matmul(grad_up, up_w)
-    grad_hidden_two = scatter_team(hidden_partial.astype(bf).reshape(4, tokens, 2, feats)).astype(
-        f32
-    )
-    grad_mixed, grad_gain_mlp = norm_backward(
+    grad_hidden_two = team_sum((grad_gate, grad_up), (gate_w, up_w), 2)
+    flat_grads = jnp.concatenate([grad_gate, grad_up], axis=2).reshape(4 * tokens, 8 * part)
+    grad_w_gate_up = left_t(flat_grads, wide_two).astype(bf).reshape(2, 4 * part, 2 * feats)
+    grad_mixed, grad_gain_mlp = fast_norm_backward(
         grad_output, grad_hidden_two, normed_two, inverse_two, gain_mlp
     )
 
     grad_mixed_b = grad_mixed.astype(bf)
-    wide_mixed = in_order(grad_mixed_b, swap_core(grad_mixed_b), c).reshape(2 * tokens, feats)
-    grad_wo_mine = left_t(wide_mixed, attended)
-    grad_wo_theirs = left_t(wide_mixed, attended_theirs)
-    sent = matmul(wide_mixed, wo_theirs).astype(bf)
+    wide_mixed = jnp.concatenate([grad_mixed_b, swap_core(grad_mixed_b)], axis=0)
+    sent = right_t(wide_mixed, wo[1]).astype(bf)
     attention_output_gradient = (
-        (matmul(wide_mixed, wo_mine) + swap_row(sent).astype(f32))
+        (right_t(wide_mixed, wo[0]) + swap_row(sent).astype(f32))
         .astype(bf)
         .reshape(seq_count, seq_len, group_heads, head_size)
     )
@@ -434,42 +1068,39 @@
         [grad_query, grad_key, grad_value.reshape(2 * tokens, head_size)], axis=1
     ).astype(bf)
     grad_qkv_theirs = swap_row(grad_qkv)
-    one_partial = right_t(grad_qkv, wq_mine) + right_t(grad_qkv_theirs, wq_theirs)
-    one_partial = one_partial.reshape(2, tokens, feats)
-    grad_hidden_one = pick(one_partial, c) + swap_core(pick(one_partial, 1 - c))
-    grad_inputs, grad_gain_attn = norm_backward(
+    one_partial = right_t(grad_qkv, wq[0]) + right_t(grad_qkv_theirs, wq[1])
+    grad_hidden_one = one_partial[:tokens] + swap_core(one_partial[tokens:])
+    grad_inputs, grad_gain_attn = fast_norm_backward(
         grad_mixed, grad_hidden_one, normed_one, inverse_one, gain_attn
     )
-    grad_gain_attn, grad_gain_mlp = lax.psum((grad_gain_attn, grad_gain_mlp), ("batch", "col"))
-
-    grad_wq = in_order(left_t(wide_one, grad_qkv), left_t(wide_one, grad_qkv_theirs), y)
-    grad_wo = in_order(grad_wo_mine, grad_wo_theirs, y)
-    grad_wa = jnp.concatenate([grad_wq, grad_wo], axis=2).astype(bf)
-    blank = jnp.zeros_like(grad_wa)
-    grad_wa = jnp.concatenate(
-        [jnp.where(c == 0, grad_wa, blank), jnp.where(c == 0, blank, grad_wa)], axis=0
-    )
-    grad_wa = lax.psum_scatter(grad_wa, "col", scatter_dimension=0, tiled=False)
-    grad_wa = lax.psum(grad_wa, "batch").astype(f32)
-    grad_w_qkv = grad_wa[:, :block_cols]
-    grad_w_out = grad_wa[:, block_cols:].T
-
-    def assemble(stacked):
-        summed = lax.psum_scatter(stacked, "col", scatter_dimension=1, tiled=True)
-        halves = summed.reshape(-1, part, 2, feats)
-        mine, theirs = pick(halves, y, 2), pick(halves, 1 - y, 2)
-        pair = in_order(mine, swap_row(theirs), y, axis=1)
-        return lax.all_gather(pair, "batch", axis=1, tiled=False).reshape(-1, ff_cols, feats)
-
-    grad_w_down = assemble(grad_w_down[None])[0].astype(f32)
-    grads = assemble(jnp.stack([grad_w_gate, grad_w_up]))
+    gains = sum_gains(jnp.stack([grad_gain_attn, grad_gain_mlp]))
+
+    grad_wq = jnp.stack([left_t(wide_one, grad_qkv), left_t(wide_one, grad_qkv_theirs)]).astype(bf)
+    grad_wo = jnp.stack([left_t(attended, wide_mixed), left_t(attended_theirs, wide_mixed)]).astype(bf)
+    grad_w_qkv, grad_w_out = sum_weights(grad_wq, grad_wo)
+
+    result = mixed_in + team_sum((activated,), (down_w,), 6)
+
+    def assemble(summed):
+        pair = jnp.stack([summed[..., :feats], swap_row(summed[..., feats:])], axis=-3)
+        pair = jnp.where(y == 0, pair, jnp.flip(pair, axis=-3))
+        sides = jnp.stack([pair, swap_chip(pair)], axis=0)
+        both = jnp.stack([sides, swap_core(sides)], axis=1)
+        first = jnp.where(lax.rem(b, 2) == 0, both, jnp.flip(both, axis=1))
+        whole = jnp.where(b < 2, first, jnp.flip(first, axis=0))
+        return whole
+
+    down_sum = lax.psum_scatter(grad_w_down, "col", scatter_dimension=0, tiled=True)
+    grad_w_down = assemble(down_sum).reshape(ff_cols, feats).astype(f32)
+    gate_up_sum = lax.psum_scatter(grad_w_gate_up, "col", scatter_dimension=1, tiled=True)
+    grads = jnp.moveaxis(assemble(gate_up_sum), 2, 0).reshape(2, ff_cols, feats)
     grad_w_gate = grads[0].T.astype(f32)
     grad_w_up = grads[1].T.astype(f32)
     return (
         result,
         grad_inputs,
-        grad_gain_attn,
-        grad_gain_mlp,
+        gains[0],
+        gains[1],
         grad_w_qkv,
         grad_w_out,
         grad_w_gate,

time: 745 us -> 510 us (0.68)
  waiting for transfers between devices: 388 us -> 98.5 us
  Pallas kernels: 0 us -> 183 us
  local copies, waits for them, and re-layouts: 123 us -> 60.6 us
  blocking collectives: 55.9 us -> 0 us
  matrix products: 91.1 us -> 51.8 us
  other arithmetic: 47.7 us -> 73.7 us
  starting transfers between devices: 12.8 us -> 22.5 us
    pallas_call x0 -> x6, Pallas kernels: none -> 183 us  [the longest x2 67.3 us: team_sum(): pl.pallas_call(functools.partial(team_sum_kernel, pairs), out_shape=jax.S...]
    all_gather x7 -> x2, waiting for transfers between devices: 158 us -> 24.2 us  [the longest x1 24.2 us: fast_shards(): gate_up_w = lax.all_gather(gate_up_w, 'col', axis=1, tiled=True)]
    reduce_scatter x5 -> x2, waiting for transfers between devices: 129 us -> 6.15 us  [the longest x1 6.13 us: fast_shards(): lax.psum_scatter(grad_w_gate_up, 'col', scatter_dimension=1, tiled=True)]
    reshape x7 -> x1, local copies, waits for them, and re-layouts: 56.2 us -> 0.28 us  [fast_shards(): attention_output_gradient = (right_t(wide_mixed, wo[0]) + swap_row(sent)....]
    psum x5 -> x0, blocking collectives: 55.9 us -> none  [the longest x1 35.4 us: fast_shards(): lax.psum((grad_gain_attn, grad_gain_mlp), ('batch', 'col'))]
    psum x1 -> x0, waiting for transfers between devices: 33.2 us -> none  [fast_shards(): grad_wa = lax.psum(grad_wa, 'batch').astype(f32)]
    dot_general x7 -> x4, matrix products: 28.7 us -> 6.8 us  [matmul(): return jnp.dot(left, right, preferred_element_type=jnp.float32)]
    ppermute x0 -> x4, waiting for transfers between devices: none -> 20.9 us  [swap_chip(): return lax.ppermute(tensor, 'batch', [(0, 2), (2, 0), (1, 3), (3, 1)])]
  transfers between devices with their start and end apart: 26 -> 30, of which waited for: 15 -> 12; matrix products, arithmetic and copies ran while one was open for 30% -> 27% of each run, Pallas kernels for 0% -> 29%
where the time goes in v2:
time: 510 us; the launch traced here: 505 us
  Pallas kernels  183 us (36%)
  waiting for transfers between devices  98.5 us (19%)
  other arithmetic  73.7 us (14%)
  local copies, waits for them, and re-layouts  60.6 us (12%)
  matrix products  51.8 us (10%)
  starting transfers between devices  22.5 us (4%)
  between operations  15.2 us (3%)
    pallas_call x2, Pallas kernels, team_sum(): pl.pallas_call(functools.partial(team_sum_kernel, pairs), out_shape=jax.S...  67.3 us
    ppermute x14, waiting for transfers between devices, swap_row(): return lax.ppermute(tensor, 'row', [(0, 1), (1, 0)])  44.8 us
    pallas_call x1, Pallas kernels, sum_weights(): pl.pallas_call(weight_sums_kernel, out_shape=(jax.ShapeDtypeStruct(grad_q...  36.4 us
    pallas_call x1, Pallas kernels, gate_up(): pl.pallas_call(gate_up_kernel, out_shape=(jax.ShapeDtypeStruct((4, tokens...  35.6 us
    pallas_call x1, Pallas kernels, gather_weights(): pl.pallas_call(weights_kernel, out_shape=(jax.ShapeDtypeStruct((2, *q), w...  30.5 us
    all_gather x1, waiting for transfers between devices, fast_shards(): gate_up_w = lax.all_gather(gate_up_w, 'col', axis=1, tiled=True)  24.2 us
    ppermute x4, waiting for transfers between devices, swap_chip(): return lax.ppermute(tensor, 'batch', [(0, 2), (2, 0), (1, 3), (3, 1)])  20.9 us
    dot_general x6, matrix products, left_t(): jnp.einsum('ta,tb->ab', left, right, preferred_element_type=jnp.float32)  20.5 us
  transfers between devices with their start and end apart: 30, of which 12 were waited for; matrix products, arithmetic and copies ran while one was open for 27% of the time, Pallas kernels for 29%

profile of v2, /device:TPU:0, one launch (start us, length us, event | category | flops | bytes accessed | tf_op | source)
XLA Modules:
  0.0 505.0 jit_solution(17132265069366499338)
XLA Ops:
  25.1 30.5 %gather_weights.1 = (bf16[2,768,384]{2,1,0:T(8,128)(2,1)S(1)}, bf16[2,192,768]{2,1,0:T(8,128)(2,1)S(1)}) custom-call(bf16[768,384]{1,0:T(8,128)(2,1)S(1)} %copy-done.3, bf16[192,768]{1,0:T(8,128)(2,1)S(1)} %copy-done.6), custom_call_target="tpu_custom_call" | custom-call | bytes 10485760 | tf_op jit(solution)/shard_map/gather_weights/pallas_call | solution.py:713
  71.2 13.0 %collective-permute-done.2 = bf16[1024,384]{0,1:T(8,128)(2,1)} collective-permute-done((bf16[1024,384]{0,1:T(8,128)(2,1)}, bf16[1024,384]{0,1:T(8,128)(2,1)}, u32[]{:S(2)}, u32[]{:S(2)}) %collective-permute-start.2) | collective-permute-done | bytes 786464 | tf_op jit(solution)/shard_map/ppermute | solution.py:903
  108.0 3.9 collective-permute-done.5
  129.2 20.0 %maximum_maximum_fusion = bf16[2048,1536]{1,0:T(8,128)(2,1)} fusion(bf16[512,768]{1,0:T(8,128)(2,1)S(1)} %get-tuple-element.40, bf16[512,768]{1,0:T(8,128)(2,1)S(1)} %get-tuple-element.41, bf16[512,768]{1,0:T(8,128)(2,1)} %collective-permute-done.12, bf16[512,768]{1,0:T(8,128)(2,1)S(1)} %collective-permute-done.11, bf16[512,768]{1,0:T(8,128)(2,1)S(1)} %get-tuple-element.42, ...), kind=kLoop, calls=%fused_computation | loop fusion | flops 50331648 | bytes 12582912 | tf_op jit(solution)/shard_map/concatenate | solution.py:983
  149.2 8.7 %fusion.80 = f32[2048,512]{1,0:T(8,128)} fusion(bf16[2048,1536]{1,0:T(8,128)(2,1)} %maximum_maximum_fusion, bf16[512,1536]{1,0:T(8,128)(2,1)} %all-gather.5.cloned.1.call-done.refs_1_), kind=kOutput, calls=%fused_computation.187 | convolution fusion | flops 3221225472 | bytes 12058624 | tf_op jit(solution)/shard_map/tb,ab->ta/dot_general | solution.py:147
  158.0 24.2 %all-gather.3.cloned.1.call-done = bf16[2,512,1536]{2,1,0:T(8,128)(2,1)} async-done(((bf16[2,128,1536]{2,1,0:T(8,128)(2,1)}), bf16[2,512,1536]{2,1,0:T(8,128)(2,1)}) %all-gather.3.cloned.1.call-update) | async-done | bytes 3145744 | tf_op jit(solution)/shard_map/all_gather | solution.py:971
  184.5 35.6 %gate_up.1 = (bf16[4,512,1536]{2,1,0:T(8,128)(2,1)}, f32[4,512,512]{2,1,0:T(8,128)}, f32[4,512,512]{2,1,0:T(8,128)}, bf16[4,512,512]{2,1,0:T(8,128)(2,1)S(1)}) custom-call(bf16[512,768]{1,0:T(8,128)(2,1)S(1)} %copy-done.2, bf16[512,1536]{1,0:T(8,128)(2,1)S(1)} %get-tuple-element.44.wg.refs_2_, bf16[512,1536]{1,0:T(8,128)(2,1)S(1)} %get-tuple-element.43.wu.refs_3_), custom_call_target="tpu_custom_call" | custom-call | flops 6442450944 | bytes 31457280 | tf_op jit(solution)/shard_map/gate_up/pallas_call | solution.py:455
  220.1 4.7 convolution_convert_fusion
  226.2 7.6 %multiply_convert_fusion = (bf16[4,512,512]{2,1,0:T(8,128)(2,1)}, bf16[4,512,512]{2,1,0:T(8,128)(2,1)}) fusion(f32[4,512,512]{2,1,0:T(8,128)} %bitcast.189, f32[4,512,512]{2,1,0:T(8,128)} %get-tuple-element.21, f32[4,512,512]{2,1,0:T(8,128)} %get-tuple-element.20), kind=kLoop, calls=%fused_computation.13 | loop fusion | flops 13631488 | bytes 16777216 | tf_op jit(solution)/shard_map/convert_element_type | solution.py:1038
  233.8 34.6 %team_sum2.1 = f32[512,768]{1,0:T(8,128)S(1)} custom-call(bf16[4,512,512]{2,1,0:T(8,128)(2,1)} %get-tuple-element.36.refs_0_, bf16[4,512,512]{2,1,0:T(8,128)(2,1)} %get-tuple-element.35.refs_1_, bf16[512,1536]{1,0:T(8,128)(2,1)S(1)} %get-tuple-element.44.wg.refs_2_, bf16[512,1536]{1,0:T(8,128)(2,1)S(1)} %get-tuple-element.43.wu.refs_3_), custom_call_target="tpu_custom_call" | custom-call | flops 6442450944 | bytes 31457280 | tf_op jit(solution)/shard_map/team_sum2/pallas_call | solution.py:608
  270.1 32.7 %team_sum1.1 = f32[512,768]{1,0:T(8,128)S(1)} custom-call(bf16[4,512,512]{2,1,0:T(8,128)(2,1)S(1)} %copy-done.9, bf16[512,1536]{1,0:T(8,128)(2,1)S(1)} %copy-done.7), custom_call_target="tpu_custom_call" | custom-call | flops 3221225472 | bytes 31457280 | tf_op jit(solution)/shard_map/team_sum1/pallas_call | solution.py:608
  306.3 10.0 %bitcast_convert_fusion = bf16[1024,1536]{1,0:T(8,128)(2,1)} fusion(bf16[4,512,1536]{2,1,0:T(8,128)(2,1)} %get-tuple-element.24, bf16[4,512,512]{2,1,0:T(8,128)(2,1)S(1)} %copy-done.26, bf16[4,512,512]{2,1,0:T(8,128)(2,1)S(1)} %copy-done.27), kind=kOutput, calls=%fused_computation.1 | convolution fusion | flops 6452412416 | bytes 13631488 | tf_op jit(solution)/shard_map/ta,tb->ab/dot_general | solution.py:143
  319.5 9.8 %collective-permute-done.16 = bf16[1024,192]{0,1:T(8,128)(2,1)} collective-permute-done((bf16[1024,192]{0,1:T(8,128)(2,1)S(1)}, bf16[1024,192]{0,1:T(8,128)(2,1)}, u32[]{:S(2)}, u32[]{:S(2)}) %collective-permute-start.16) | collective-permute-done | bytes 393248 | tf_op jit(solution)/shard_map/ppermute | solution.py:903
  346.3 13.7 %collective-permute-done.17 = bf16[1024,384]{0,1:T(8,128)(2,1)S(1)} collective-permute-done((bf16[1024,384]{0,1:T(8,128)(2,1)S(1)}, bf16[1024,384]{0,1:T(8,128)(2,1)S(1)}, u32[]{:S(2)}, u32[]{:S(2)}) %collective-permute-start.17) | collective-permute-done | bytes 786464 | tf_op jit(solution)/shard_map/ppermute | solution.py:903
  368.4 6.1 %reduce-scatter.3.cloned.1.call-done = bf16[2,128,1536]{2,1,0:T(8,128)(2,1)} async-done(((bf16[2,512,1536]{2,1,0:T(8,128)(2,1)}), bf16[2,128,1536]{2,1,0:T(8,128)(2,1)}) %reduce-scatter.3.cloned.1.call-update) | async-done | bytes 786448 | tf_op jit(solution)/shard_map/reduce_scatter | solution.py:1095
  377.4 36.4 %sum_weights.1 = (f32[768,384]{1,0:T(8,128)S(1)}, f32[192,768]{1,0:T(8,128)S(1)}) custom-call(bf16[2,768,384]{2,1,0:T(8,128)(2,1)S(1)} %pad_maximum_fusion.6.gq, bf16[2,192,768]{2,1,0:T(8,128)(2,1)S(1)} %pad_maximum_fusion.10.go), custom_call_target="tpu_custom_call" | custom-call | bytes 10485760 | tf_op jit(solution)/shard_map/sum_weights/pallas_call | solution.py:820
  418.5 7.5 %collective-permute-done.24 = bf16[2,128,768]{2,1,0:T(8,128)(2,1)S(1)} collective-permute-done((bf16[2,128,768]{2,1,0:T(8,128)(2,1)S(1)}, bf16[2,128,768]{2,1,0:T(8,128)(2,1)S(1)}, u32[]{:S(2)}, u32[]{:S(2)}) %collective-permute-start.24) | collective-permute-done | bytes 393248 | tf_op jit(solution)/shard_map/ppermute | solution.py:911
  427.4 13.3 %collective-permute-done.21 = bf16[2,2,128,768]{3,2,0,1:T(8,128)(2,1)S(1)} collective-permute-done((bf16[2,2,128,768]{3,2,0,1:T(8,128)(2,1)S(1)}, bf16[2,2,128,768]{3,2,0,1:T(8,128)(2,1)S(1)}, u32[]{:S(2)}, u32[]{:S(2)}) %collective-permute-start.21) | collective-permute-done | bytes 786464 | tf_op jit(solution)/shard_map/ppermute | solution.py:911
  443.2 12.8 %sum_gains.1 = f32[2,768]{1,0:T(2,128)} custom-call(f32[2,768]{1,0:T(2,128)} %pad_maximum_fusion.18.part), custom_call_target="tpu_custom_call" | custom-call | tf_op jit(solution)/shard_map/sum_gains/pallas_call | solution.py:883
  459.7 4.0 multiply_add_fusion
  473.9 5.7 %copy.63 = f32[1,2,2,2,128,768]{4,3,2,1,5,0:T(2,128)} copy(f32[1,2,2,2,128,768]{5,4,0,3,1,2:T(8,128)} %get-tuple-element.37) | data formatting | bytes 6291456 | tf_op jit(solution)/shard_map/convert_element_type | solution.py:1098
  479.7 5.5 %reshape.127 = f32[1024,768]{0,1:T(8,128)} reshape(f32[1,2,2,2,128,768]{4,3,2,1,5,0:T(2,128)} %copy.63) | data formatting | bytes 6291456 | tf_op jit(solution)/shard_map/convert_element_type | solution.py:1098
  485.1 5.7 %copy.62 = f32[1,2,2,2,128,768]{4,3,2,1,5,0:T(2,128)} copy(f32[1,2,2,2,128,768]{5,4,0,3,1,2:T(8,128)} %get-tuple-element.38) | data formatting | bytes 6291456 | tf_op jit(solution)/shard_map/convert_element_type | solution.py:1097
  490.9 5.5 %reshape.126 = f32[1024,768]{0,1:T(8,128)} reshape(f32[1,2,2,2,128,768]{4,3,2,1,5,0:T(2,128)} %copy.62) | data formatting | bytes 6291456 | tf_op jit(solution)/shard_map/convert_element_type | solution.py:1097
  (281 shorter events, 138.0 us)
Async XLA Ops:
  7.2 142.0 %all-gather.5.cloned.1.call-start = ((), (), s32[]{:S(2)}) async-start(), calls=%async_computation.3 | async-start | bytes 1966080 | tf_op jit(solution)/shard_map/all_gather | solution.py:972
  14.4 90.0 %collective-permute-start.11 = (bf16[512,768]{1,0:T(8,128)(2,1)}, bf16[512,768]{1,0:T(8,128)(2,1)S(1)}, u32[]{:S(2)}, u32[]{:S(2)}) collective-permute-start(bf16[512,768]{1,0:T(8,128)(2,1)} %convert_element_type.105), channel_id=1, source_target_pairs={{0,16},{16,0},{8,24},{24,8},{1,17},{17,1},{9,25},{25,9},{2,18},{18... | collective-permute-start | bytes 2359304 | tf_op jit(solution)/shard_map/ppermute | solution.py:911
  15.9 53.6 %collective-permute-start.10 = (bf16[512,768]{1,0:T(8,128)(2,1)}, bf16[512,768]{1,0:T(8,128)(2,1)}, u32[]{:S(2)}, u32[]{:S(2)}) collective-permute-start(bf16[512,768]{1,0:T(8,128)(2,1)} %convert_element_type.105), channel_id=1, source_target_pairs={{0,4},{4,0},{1,5},{5,1},{2,6},{6,2},{3,7},{7,3},{8,12},{12,8},{9,1... | collective-permute-start | bytes 2359304 | tf_op jit(solution)/shard_map/ppermute | solution.py:903
  17.5 42.9 %collective-permute-start.1 = (bf16[512,768]{1,0:T(8,128)(2,1)}, bf16[512,768]{1,0:T(8,128)(2,1)}, u32[]{:S(2)}, u32[]{:S(2)}) collective-permute-start(bf16[512,768]{1,0:T(8,128)(2,1)} %multiply_convert_fusion.3), channel_id=1, source_target_pairs={{0,8},{8,0},{16,24},{24,16},{1,9},{9,1},{17,25},{25,17},{2,10},{10... | collective-permute-start | bytes 2359304 | tf_op jit(solution)/shard_map/ppermute | solution.py:907
  17.5 47.5 %collective-permute-start.3 = (s32[2,2,512]{2,0,1:T(2,128)S(1)}, s32[2,2,512]{2,0,1:T(2,128)S(1)}, u32[]{:S(2)}, u32[]{:S(2)}) collective-permute-start(s32[2,2,512]{2,0,1:T(2,128)S(1)} %pad_add_fusion), channel_id=1, source_target_pairs={{0,4},{4,0},{1,5},{5,1},{2,6},{6,2},{3,7},{7,3},{8,12},{12,8},{9,1... | collective-permute-start | bytes 24584 | tf_op jit(solution)/shard_map/ppermute | solution.py:903
  20.9 46.4 %collective-permute-start.9 = (bf16[128,768]{1,0:T(8,128)(2,1)}, bf16[128,768]{1,0:T(8,128)(2,1)}, u32[]{:S(2)}, u32[]{:S(2)}) collective-permute-start(bf16[128,768]{1,0:T(8,128)(2,1)} %get-tuple-element.49), channel_id=1, source_target_pairs={{0,4},{4,0},{1,5},{5,1},{2,6},{6,2},{3,7},{7,3},{8,12},{12,8},{9,1... | collective-permute-start | bytes 589832 | tf_op jit(solution)/shard_map/ppermute | solution.py:903
  63.5 20.7 %collective-permute-start.2 = (bf16[1024,384]{0,1:T(8,128)(2,1)}, bf16[1024,384]{0,1:T(8,128)(2,1)}, u32[]{:S(2)}, u32[]{:S(2)}) collective-permute-start(bf16[1024,384]{0,1:T(8,128)(2,1)} %convolution_convert_fusion.1), channel_id=1, source_target_pairs={{0,4},{4,0},{1,5},{5,1},{2,6},{6,2},{3,7},{7,3},{8,12},{12,8},{9,1... | collective-permute-start | bytes 2359304 | tf_op jit(solution)/shard_map/ppermute | solution.py:903
  66.3 50.3 %collective-permute-start.8 = (bf16[2,128,768]{2,1,0:T(8,128)(2,1)}, bf16[2,128,768]{2,1,0:T(8,128)(2,1)}, u32[]{:S(2)}, u32[]{:S(2)}) collective-permute-start(bf16[2,128,768]{2,1,0:T(8,128)(2,1)} %pad_maximum_fusion.12), channel_id=1, source_target_pairs={{0,4},{4,0},{1,5},{5,1},{2,6},{6,2},{3,7},{7,3},{8,12},{12,8},{9,1... | collective-permute-start | bytes 1179656 | tf_op jit(solution)/shard_map/ppermute | solution.py:903
  69.2 113.0 %all-gather.3.cloned.1.call-start = ((), (), s32[]{:S(2)}) async-start(), calls=%async_computation.2 | async-start | bytes 3932160 | tf_op jit(solution)/shard_map/all_gather | solution.py:971
  69.5 34.9 %collective-permute-start.12 = (bf16[512,768]{1,0:T(8,128)(2,1)}, bf16[512,768]{1,0:T(8,128)(2,1)}, u32[]{:S(2)}, u32[]{:S(2)}) collective-permute-start(bf16[512,768]{1,0:T(8,128)(2,1)} %collective-permute-done.10), channel_id=1, source_target_pairs={{0,16},{16,0},{8,24},{24,8},{1,17},{17,1},{9,25},{25,9},{2,18},{18... | collective-permute-start | bytes 2359304 | tf_op jit(solution)/shard_map/ppermute | solution.py:911
  107.4 19.6 %collective-permute-start.13 = (bf16[4,512,768]{2,1,0:T(8,128)(2,1)}, bf16[4,512,768]{2,1,0:T(8,128)(2,1)}, u32[]{:S(2)}, u32[]{:S(2)}) collective-permute-start(bf16[4,512,768]{2,1,0:T(8,128)(2,1)} %pad_maximum_fusion), channel_id=1, source_target_pairs={{0,8},{8,0},{16,24},{24,16},{1,9},{9,1},{17,25},{25,17},{2,10},{10... | collective-permute-start | bytes 9437192 | tf_op jit(solution)/shard_map/ppermute | solution.py:907
  118.7 247.7 %reduce-scatter.5.cloned.1.call-start = ((), (), s32[]{:S(2)}) async-start(), calls=%async_computation.5 | async-start | bytes 1966080 | tf_op jit(solution)/shard_map/reduce_scatter | solution.py:1093
  226.2 148.4 %reduce-scatter.3.cloned.1.call-start = ((), (), s32[]{:S(2)}) async-start(), calls=%async_computation.4 | async-start | bytes 3932160 | tf_op jit(solution)/shard_map/reduce_scatter | solution.py:1095
  268.9 34.0 %collective-permute-start.14 = (f32[512]{0:T(512)S(1)}, f32[512]{0:T(512)S(1)}, u32[]{:S(2)}, u32[]{:S(2)}) collective-permute-start(f32[512]{0:T(512)S(1)} %get-tuple-element.28), channel_id=1, source_target_pairs={{0,4},{4,0},{1,5},{5,1},{2,6},{6,2},{3,7},{7,3},{8,12},{12,8},{9,1... | collective-permute-start | bytes 6152 | tf_op jit(solution)/shard_map/ppermute | solution.py:903
  305.1 11.3 %collective-permute-start.15 = (bf16[512,768]{1,0:T(8,128)(2,1)S(1)}, bf16[512,768]{1,0:T(8,128)(2,1)S(1)}, u32[]{:S(2)}, u32[]{:S(2)}) collective-permute-start(bf16[512,768]{1,0:T(8,128)(2,1)S(1)} %get-tuple-element.31), channel_id=1, source_target_pairs={{0,8},{8,0},{16,24},{24,16},{1,9},{9,1},{17,25},{25,17},{2,10},{10... | collective-permute-start | bytes 2359304 | tf_op jit(solution)/shard_map/ppermute | solution.py:907
  318.0 11.3 %collective-permute-start.16 = (bf16[1024,192]{0,1:T(8,128)(2,1)S(1)}, bf16[1024,192]{0,1:T(8,128)(2,1)}, u32[]{:S(2)}, u32[]{:S(2)}) collective-permute-start(bf16[1024,192]{0,1:T(8,128)(2,1)S(1)} %convolution_convert_fusion.4), channel_id=1, source_target_pairs={{0,4},{4,0},{1,5},{5,1},{2,6},{6,2},{3,7},{7,3},{8,12},{12,8},{9,1... | collective-permute-start | bytes 1179656 | tf_op jit(solution)/shard_map/ppermute | solution.py:903
  341.3 18.8 %collective-permute-start.17 = (bf16[1024,384]{0,1:T(8,128)(2,1)S(1)}, bf16[1024,384]{0,1:T(8,128)(2,1)S(1)}, u32[]{:S(2)}, u32[]{:S(2)}) collective-permute-start(bf16[1024,384]{0,1:T(8,128)(2,1)S(1)} %constant_dynamic-update-slice_fusion), channel_id=1, source_target_pairs={{0,4},{4,0},{1,5},{5,1},{2,6},{6,2},{3,7},{7,3},{8,12},{12,8},{9,1... | collective-permute-start | bytes 2359304 | tf_op jit(solution)/shard_map/ppermute | solution.py:903
  364.0 52.5 %collective-permute-start.18 = (f32[512,768]{1,0:T(8,128)}, f32[512,768]{1,0:T(8,128)}, u32[]{:S(2)}, u32[]{:S(2)}) collective-permute-start(f32[512,768]{1,0:T(8,128)} %slice.169), channel_id=1, source_target_pairs={{0,8},{8,0},{16,24},{24,16},{1,9},{9,1},{17,25},{25,17},{2,10},{10... | collective-permute-start | bytes 4718600 | tf_op jit(solution)/shard_map/ppermute | solution.py:907
  367.5 46.3 %collective-permute-start.23 = (bf16[128,768]{1,0:T(8,128)(2,1)S(1)}, bf16[128,768]{1,0:T(8,128)(2,1)S(1)}, u32[]{:S(2)}, u32[]{:S(2)}) collective-permute-start(bf16[128,768]{1,0:T(8,128)(2,1)S(1)} %get-tuple-element.69), channel_id=1, source_target_pairs={{0,4},{4,0},{1,5},{5,1},{2,6},{6,2},{3,7},{7,3},{8,12},{12,8},{9,1... | collective-permute-start | bytes 589832 | tf_op jit(solution)/shard_map/ppermute | solution.py:903
  375.7 38.8 %collective-permute-start.20 = (bf16[2,128,768]{2,1,0:T(8,128)(2,1)S(1)}, bf16[2,128,768]{2,1,0:T(8,128)(2,1)S(1)}, u32[]{:S(2)}, u32[]{:S(2)}) collective-permute-start(bf16[2,128,768]{2,1,0:T(8,128)(2,1)S(1)} %get-tuple-element.61), channel_id=1, source_target_pairs={{0,4},{4,0},{1,5},{5,1},{2,6},{6,2},{3,7},{7,3},{8,12},{12,8},{9,1... | collective-permute-start | bytes 1179656 | tf_op jit(solution)/shard_map/ppermute | solution.py:903
  414.0 12.1 %collective-permute-start.24 = (bf16[2,128,768]{2,1,0:T(8,128)(2,1)S(1)}, bf16[2,128,768]{2,1,0:T(8,128)(2,1)S(1)}, u32[]{:S(2)}, u32[]{:S(2)}) collective-permute-start(bf16[2,128,768]{2,1,0:T(8,128)(2,1)S(1)} %reverse_select_fusion.5), channel_id=1, source_target_pairs={{0,16},{16,0},{8,24},{24,8},{1,17},{17,1},{9,25},{25,9},{2,18},{18... | collective-permute-start | bytes 1179656 | tf_op jit(solution)/shard_map/ppermute | solution.py:911
  414.7 26.0 %collective-permute-start.21 = (bf16[2,2,128,768]{3,2,0,1:T(8,128)(2,1)S(1)}, bf16[2,2,128,768]{3,2,0,1:T(8,128)(2,1)S(1)}, u32[]{:S(2)}, u32[]{:S(2)}) collective-permute-start(bf16[2,2,128,768]{3,2,0,1:T(8,128)(2,1)S(1)} %reverse_select_fusion.4), channel_id=1, source_target_pairs={{0,16},{16,0},{8,24},{24,8},{1,17},{17,1},{9,25},{25,9},{2,18},{18... | collective-permute-start | bytes 2359304 | tf_op jit(solution)/shard_map/ppermute | solution.py:911
  427.3 36.4 %collective-permute-start.25 = (bf16[2,2,128,768]{3,2,1,0:T(8,128)(2,1)}, bf16[2,2,128,768]{3,2,1,0:T(8,128)(2,1)}, u32[]{:S(2)}, u32[]{:S(2)}) collective-permute-start(bf16[2,2,128,768]{3,2,1,0:T(8,128)(2,1)} %get-tuple-element.59), channel_id=1, source_target_pairs={{0,8},{8,0},{16,24},{24,16},{1,9},{9,1},{17,25},{25,17},{2,10},{10... | collective-permute-start | bytes 2359304 | tf_op jit(solution)/shard_map/ppermute | solution.py:907
  442.6 25.0 %collective-permute-start.22 = (bf16[2,2,2,128,768]{4,3,1,2,0:T(8,128)(2,1)}, bf16[2,2,2,128,768]{4,3,1,2,0:T(8,128)(2,1)}, u32[]{:S(2)}, u32[]{:S(2)}) collective-permute-start(bf16[2,2,2,128,768]{4,3,1,2,0:T(8,128)(2,1)} %get-tuple-element.46), channel_id=1, source_target_pairs={{0,8},{8,0},{16,24},{24,16},{1,9},{9,1},{17,25},{25,17},{2,10},{10... | collective-permute-start | bytes 4718600 | tf_op jit(solution)/shard_map/ppermute | solution.py:907
  (65 other events, 551.8 us)
Sparse Core Ops, SparseCore 0:
  69.3 36.2 all-gather.4
  118.8 63.3 all-gather.2
  226.3 33.3 reduce-scatter.4
  316.4 58.0 reduce-scatter.2
